TPU v7x, 16 devices: a 4x2x1 block of a 4x4x8 slice. The times are simulated.
16 devices in a mesh: dp: 2 (over y, z), gp: 8 (over x, core).
Axes of the slice: x: 4, y: 2, z: 1, core: 2. Of those that a mesh axis runs over, the one named last changes fastest.
The devices are a block of a 4x4x8 slice.
Arguments:
- x_prev: float32 [65536, 78], P(('dp', 'gp')), parts along dimension 0
- x_cur: float32 [65536, 78], P(('dp', 'gp')), parts along dimension 0
- forcing: float32 [65536, 2, 3], P(('dp', 'gp')), parts along dimension 0
- grid_static: float32 [65536, 3], P(('dp', 'gp')), parts along dimension 0
- g2m_feat: float32 [65536, 4], P(('dp', 'gp')), parts along dimension 0
- m2g_feat: float32 [65536, 4], P(('dp', 'gp')), parts along dimension 0
- mesh_feat: float32 [16384, 3], P(('dp', 'gp')), parts along dimension 0
- mesh_edge_feat: float32 [16384, 6, 4], P(('dp', 'gp')), parts along dimension 0
- norm_stats: float32 [4, 78], replicated
- w_grid_in: bfloat16 [162, 256], replicated
- w_mesh_in: bfloat16 [3, 256], replicated
- w_eemb_in: bfloat16 [3, 4, 256], replicated
- w_embed_out: bfloat16 [5, 256, 256], replicated
- w_edge_in: bfloat16 [18, 768, 256], replicated
- w_edge_out: bfloat16 [18, 256, 256], replicated
- w_node_in: bfloat16 [18, 512, 256], replicated
- w_node_out: bfloat16 [18, 256, 256], replicated
- w_grid_self: bfloat16 [2, 256, 256], replicated
- w_out_hidden: bfloat16 [256, 256], replicated
- w_out_final: bfloat16 [256, 78], replicated
Outputs:
- output 1: float32 [65536, 78], P(('dp', 'gp')), parts along dimension 0
- output 2: float32 [65536, 78], P(('dp', 'gp')), parts along dimension 0
There are 2 independent parts. A program takes and returns all parts, laid end to end along the dimension named above; an argument that names none is the same for every part.
All inputs are finite; a program needn't handle non-finite values.
Results may differ from a plain program's by a relative error of at most 0.00876042.
Values are sent between devices in bfloat16 or wider.
A program may use at most 768 MiB of HBM per device.

v0:
```python
import jax
import jax.numpy as jnp
from jax import lax
from jax.sharding import PartitionSpec as P


def layer_norm(values):
    centre = jnp.mean(values, axis=-1, keepdims=True)
    centred = values - centre
    spread = jnp.mean(centred * centred, axis=-1, keepdims=True)
    return centred * lax.rsqrt(spread + 1e-5)


def matmul_f32(values, weight):
    return jnp.dot(values, weight, preferred_element_type=jnp.float32)


def mlp_tail(pre_act, w_second):
    hidden = jax.nn.silu(pre_act).astype(jnp.bfloat16)
    return layer_norm(matmul_f32(hidden, w_second))


def residual(base, update):
    return (base.astype(jnp.float32) + update).astype(jnp.bfloat16)


def embed_static(features, w_first, w_second):
    return mlp_tail(matmul_f32(features.astype(jnp.bfloat16), w_first), w_second).astype(jnp.bfloat16)


def solution(mesh):
    group_size = mesh.shape["gp"]
    quarter_hop = group_size // 4
    row_spec = P(("dp", "gp"))
    edge_spec = P(("dp", "gp"), None, None)
    whole = P()

    def shift_pairs(hop_count):
        return [(source, (source + hop_count) % group_size) for source in range(group_size)]

    def local_run(x_prev, x_cur, forcing, grid_static, g2m_feat, m2g_feat, mesh_feat, mesh_edge_feat, norm_stats, w_grid_in, w_mesh_in, w_eemb_in, w_embed_out, w_edge_in, w_edge_out, w_node_in, w_node_out, w_grid_self, w_out_hidden, w_out_final):
        grid_dev = x_prev.shape[0]
        mesh_dev = mesh_feat.shape[0]
        grid_ratio = grid_dev // mesh_dev
        half_shard = mesh_dev // 2
        half_rows = half_shard * grid_ratio
        latent = w_embed_out.shape[-1]
        blocks = w_edge_in.shape[0]
        mesh_lat = embed_static(mesh_feat, w_mesh_in, w_embed_out[1])
        g2m_lat = embed_static(g2m_feat, w_eemb_in[0], w_embed_out[2])
        m2g_lat = embed_static(m2g_feat, w_eemb_in[1], w_embed_out[3])
        edge_base = embed_static(mesh_edge_feat, w_eemb_in[2], w_embed_out[4])
        in_mean = norm_stats[0]
        in_std = norm_stats[1]
        diff_mean = norm_stats[2]
        diff_std = norm_stats[3]
        state_prev = x_prev
        state_cur = x_cur
        outputs = []
        for step_idx in range(2):
            features = jnp.concatenate([(state_prev - in_mean) / in_std, (state_cur - in_mean) / in_std, forcing[:, step_idx, :], grid_static], axis=1)
            grid_lat = embed_static(features, w_grid_in, w_embed_out[0])
            from_prev = lax.ppermute(grid_lat[grid_dev - half_rows:], "gp", shift_pairs(1))
            senders = jnp.concatenate([from_prev, grid_lat[:grid_dev - half_rows]], axis=0)
            w_first = w_edge_in[0]
            recv_term = matmul_f32(mesh_lat, w_first[2 * latent:])
            pre_act = matmul_f32(g2m_lat, w_first[:latent]) + matmul_f32(senders, w_first[latent:2 * latent])
            pre_act = (pre_act.reshape(mesh_dev, grid_ratio, latent) + recv_term[:, None, :]).reshape(grid_dev, latent)
            enc_edge = residual(g2m_lat, mlp_tail(pre_act, w_edge_out[0]))
            enc_sum = jnp.sum(enc_edge.reshape(mesh_dev, grid_ratio, latent), axis=1, dtype=jnp.float32).astype(jnp.bfloat16)
            node_w = w_node_in[0]
            mesh_cur = residual(mesh_lat, mlp_tail(matmul_f32(mesh_lat, node_w[:latent]) + matmul_f32(enc_sum, node_w[latent:]), w_node_out[0]))
            grid_cur = residual(grid_lat, mlp_tail(matmul_f32(grid_lat, w_grid_self[0]), w_grid_self[1]))
            edge_lat = edge_base
            for layer_idx in range(1, blocks - 1):
                prev_tail = lax.ppermute(mesh_cur[mesh_dev - half_shard:], "gp", shift_pairs(1))
                next_head = lax.ppermute(mesh_cur[:half_shard], "gp", shift_pairs(-1))
                far_plus = lax.ppermute(mesh_cur, "gp", shift_pairs(-quarter_hop))
                far_minus = lax.ppermute(mesh_cur, "gp", shift_pairs(quarter_hop))
                w_layer = w_edge_in[layer_idx]
                extended = jnp.concatenate([prev_tail, mesh_cur, next_head, far_plus, far_minus], axis=0)
                send_proj = matmul_f32(extended, w_layer[latent:2 * latent])
                send_term = jnp.stack([
                    send_proj[half_shard + 1:half_shard + 1 + mesh_dev],
                    send_proj[half_shard - 1:half_shard - 1 + mesh_dev],
                    send_proj[2 * half_shard:2 * half_shard + mesh_dev],
                    send_proj[:mesh_dev],
                    send_proj[2 * mesh_dev:3 * mesh_dev],
                    send_proj[3 * mesh_dev:4 * mesh_dev]], axis=1)
                recv_term = matmul_f32(mesh_cur, w_layer[2 * latent:])
                pre_act = jnp.einsum("nkc,cd->nkd", edge_lat, w_layer[:latent], preferred_element_type=jnp.float32) + send_term + recv_term[:, None, :]
                edge_lat = residual(edge_lat, mlp_tail(pre_act, w_edge_out[layer_idx]))
                edge_sum = jnp.sum(edge_lat, axis=1, dtype=jnp.float32).astype(jnp.bfloat16)
                node_w = w_node_in[layer_idx]
                mesh_cur = residual(mesh_cur, mlp_tail(matmul_f32(mesh_cur, node_w[:latent]) + matmul_f32(edge_sum, node_w[latent:]), w_node_out[layer_idx]))
            head_next = lax.ppermute(mesh_cur[:half_shard], "gp", shift_pairs(-1))
            mesh_send = jnp.concatenate([mesh_cur[half_shard:], head_next], axis=0)
            w_last = w_edge_in[blocks - 1]
            send_term = matmul_f32(mesh_send, w_last[latent:2 * latent])
            pre_act = matmul_f32(m2g_lat, w_last[:latent]) + matmul_f32(grid_cur, w_last[2 * latent:])
            pre_act = (pre_act.reshape(mesh_dev, grid_ratio, latent) + send_term[:, None, :]).reshape(grid_dev, latent)
            dec_edge = residual(m2g_lat, mlp_tail(pre_act, w_edge_out[blocks - 1]))
            node_w = w_node_in[blocks - 1]
            grid_out = residual(grid_cur, mlp_tail(matmul_f32(grid_cur, node_w[:latent]) + matmul_f32(dec_edge, node_w[latent:]), w_node_out[blocks - 1]))
            hidden = jax.nn.silu(matmul_f32(grid_out, w_out_hidden)).astype(jnp.bfloat16)
            prediction = matmul_f32(hidden, w_out_final)
            state_next = state_cur + diff_std * prediction + diff_mean
            outputs.append(state_next)
            state_prev, state_cur = state_cur, state_next
        return outputs[0], outputs[1]

    in_specs = (row_spec, row_spec, edge_spec, row_spec, row_spec, row_spec, row_spec, edge_spec, whole) + (whole,) * 11
    return jax.shard_map(local_run, mesh=mesh, in_specs=in_specs, out_specs=(row_spec, row_spec), check_vma=False)
```

profile of v0, /device:TPU:113, one launch (start us, length us, event | category | flops | bytes accessed | tf_op | source)
XLA Modules:
  0.0 1903.3 jit_solution(15713840562552205760)
XLA Ops:
  85.2 19.9 %fusion.1405 = (f32[4096]{0:T(1024)S(1)}, f32[4096,256]{1,0:T(8,128)}) fusion(bf16[18,256,256]{2,1,0:T(8,128)(2,1)} %param.34, f32[4096,256]{1,0:T(8,128)} %add.1659, f32[4096,256]{1,0:T(8,128)} %fusion.846, bf16[2048,256]{0,1:T(8,128)(2,1)S(1)} %get-tuple-element.65, bf16[2048,256]{0,1:T(8,128)(2,1)} %collective-permute-done, ...), kind=kOutput, calls=%fused_computation.1984 | convolution fusion | flops 1086320640 | bytes 14958592 | tf_op jit(solution)/shard_map/dot_general | solution.py:15
  131.0 11.5 collective-permute-done.1
  164.8 9.0 collective-permute-done.5
  186.4 10.2 fusion.1422
  217.5 8.3 collective-permute-done.9
  238.4 9.8 fusion.1428
  269.6 8.3 collective-permute-done.13
  290.5 9.8 fusion.1434
  342.6 9.8 fusion.1440
  373.6 8.3 collective-permute-done.21
  394.5 10.2 fusion.1446
  446.8 9.8 fusion.1452
  498.9 9.8 fusion.1458
  529.9 8.3 collective-permute-done.33
  550.9 10.0 fusion.1464
  603.0 10.2 fusion.1470
  655.3 9.8 fusion.1476
  686.4 8.3 collective-permute-done.45
  707.4 9.8 fusion.1482
  759.3 10.0 fusion.1488
  811.4 9.8 fusion.1494
  863.7 9.8 fusion.1500
  915.7 9.8 fusion.1506
  1080.1 9.1 collective-permute-done.71
  1101.9 10.0 fusion.1536
  1153.7 9.8 fusion.1542
  1206.1 9.8 fusion.1548
  1237.2 8.3 collective-permute-done.83
  1258.3 9.8 fusion.1554
  1289.4 8.3 collective-permute-done.87
  1310.4 10.0 fusion.1560
  1362.6 9.8 fusion.1566
  1394.1 8.3 collective-permute-done.95
  1415.1 9.8 fusion.1572
  1446.1 8.3 collective-permute-done.99
  1467.1 10.0 fusion.1578
  1498.3 8.3 collective-permute-done.103
  1519.3 10.0 fusion.1584
  1550.6 8.3 collective-permute-done.107
  1571.5 9.8 fusion.1590
  1623.9 9.8 fusion.1596
  1655.0 8.3 collective-permute-done.115
  1676.0 10.0 fusion.1602
  1707.2 8.3 collective-permute-done.119
  1728.2 9.8 fusion.1608
  1759.5 8.3 collective-permute-done.123
  1780.5 9.8 fusion.1614
  1832.5 9.8 fusion.1620
  (1300 shorter events, 1436.1 us)
Async XLA Ops:
  17.0 68.2 %collective-permute-start = (bf16[2048,256]{0,1:T(8,128)(2,1)}, bf16[2048,256]{0,1:T(8,128)(2,1)}, u32[]{:S(2)}, u32[]{:S(2)}) collective-permute-start(bf16[2048,256]{0,1:T(8,128)(2,1)} %get-tuple-element.64), channel_id=1, source_target_pairs={{0,1},{1,2},{2,3},{3,4},{4,5},{5,6},{6,7},{7,0},{8,9},{9,10},{10,1... | collective-permute-start | bytes 3145736 | tf_op jit(solution)/shard_map/ppermute | solution.py:63
  156.7 19.4 %collective-permute-start.7 = (bf16[1024,256]{1,0:T(8,128)(2,1)S(1)}, bf16[1024,256]{1,0:T(8,128)(2,1)S(1)}, u32[]{:S(2)}, u32[]{:S(2)}) collective-permute-start(bf16[1024,256]{1,0:T(8,128)(2,1)S(1)} %add_convert_fusion.75), channel_id=1, source_target_pairs={{0,6},{1,7},{2,0},{3,1},{4,2},{5,3},{6,4},{7,5},{8,14},{9,15},{10,... | collective-permute-start | bytes 1572872 | tf_op jit(solution)/shard_map/ppermute | solution.py:78
  159.5 17.5 collective-permute-start.8
  208.8 19.2 %collective-permute-start.11 = (bf16[1024,256]{1,0:T(8,128)(2,1)S(1)}, bf16[1024,256]{1,0:T(8,128)(2,1)S(1)}, u32[]{:S(2)}, u32[]{:S(2)}) collective-permute-start(bf16[1024,256]{1,0:T(8,128)(2,1)S(1)} %add_convert_fusion.74), channel_id=1, source_target_pairs={{0,6},{1,7},{2,0},{3,1},{4,2},{5,3},{6,4},{7,5},{8,14},{9,15},{10,... | collective-permute-start | bytes 1572872 | tf_op jit(solution)/shard_map/ppermute | solution.py:78
  260.6 19.6 %collective-permute-start.15 = (bf16[1024,256]{1,0:T(8,128)(2,1)S(1)}, bf16[1024,256]{1,0:T(8,128)(2,1)S(1)}, u32[]{:S(2)}, u32[]{:S(2)}) collective-permute-start(bf16[1024,256]{1,0:T(8,128)(2,1)S(1)} %add_convert_fusion.73), channel_id=1, source_target_pairs={{0,6},{1,7},{2,0},{3,1},{4,2},{5,3},{6,4},{7,5},{8,14},{9,15},{10,... | collective-permute-start | bytes 1572872 | tf_op jit(solution)/shard_map/ppermute | solution.py:78
  312.5 19.6 %collective-permute-start.19 = (bf16[1024,256]{1,0:T(8,128)(2,1)S(1)}, bf16[1024,256]{1,0:T(8,128)(2,1)S(1)}, u32[]{:S(2)}, u32[]{:S(2)}) collective-permute-start(bf16[1024,256]{1,0:T(8,128)(2,1)S(1)} %add_convert_fusion.72), channel_id=1, source_target_pairs={{0,6},{1,7},{2,0},{3,1},{4,2},{5,3},{6,4},{7,5},{8,14},{9,15},{10,... | collective-permute-start | bytes 1572872 | tf_op jit(solution)/shard_map/ppermute | solution.py:78
  364.6 19.6 %collective-permute-start.23 = (bf16[1024,256]{1,0:T(8,128)(2,1)S(1)}, bf16[1024,256]{1,0:T(8,128)(2,1)S(1)}, u32[]{:S(2)}, u32[]{:S(2)}) collective-permute-start(bf16[1024,256]{1,0:T(8,128)(2,1)S(1)} %add_convert_fusion.71), channel_id=1, source_target_pairs={{0,6},{1,7},{2,0},{3,1},{4,2},{5,3},{6,4},{7,5},{8,14},{9,15},{10,... | collective-permute-start | bytes 1572872 | tf_op jit(solution)/shard_map/ppermute | solution.py:78
  367.9 17.1 collective-permute-start.24
  416.9 19.6 %collective-permute-start.27 = (bf16[1024,256]{1,0:T(8,128)(2,1)S(1)}, bf16[1024,256]{1,0:T(8,128)(2,1)S(1)}, u32[]{:S(2)}, u32[]{:S(2)}) collective-permute-start(bf16[1024,256]{1,0:T(8,128)(2,1)S(1)} %add_convert_fusion.70), channel_id=1, source_target_pairs={{0,6},{1,7},{2,0},{3,1},{4,2},{5,3},{6,4},{7,5},{8,14},{9,15},{10,... | collective-permute-start | bytes 1572872 | tf_op jit(solution)/shard_map/ppermute | solution.py:78
  469.0 19.6 %collective-permute-start.31 = (bf16[1024,256]{1,0:T(8,128)(2,1)S(1)}, bf16[1024,256]{1,0:T(8,128)(2,1)S(1)}, u32[]{:S(2)}, u32[]{:S(2)}) collective-permute-start(bf16[1024,256]{1,0:T(8,128)(2,1)S(1)} %add_convert_fusion.69), channel_id=1, source_target_pairs={{0,6},{1,7},{2,0},{3,1},{4,2},{5,3},{6,4},{7,5},{8,14},{9,15},{10,... | collective-permute-start | bytes 1572872 | tf_op jit(solution)/shard_map/ppermute | solution.py:78
  520.9 19.6 %collective-permute-start.35 = (bf16[1024,256]{1,0:T(8,128)(2,1)S(1)}, bf16[1024,256]{1,0:T(8,128)(2,1)S(1)}, u32[]{:S(2)}, u32[]{:S(2)}) collective-permute-start(bf16[1024,256]{1,0:T(8,128)(2,1)S(1)} %add_convert_fusion.68), channel_id=1, source_target_pairs={{0,6},{1,7},{2,0},{3,1},{4,2},{5,3},{6,4},{7,5},{8,14},{9,15},{10,... | collective-permute-start | bytes 1572872 | tf_op jit(solution)/shard_map/ppermute | solution.py:78
  524.2 17.1 collective-permute-start.36
  573.1 19.6 %collective-permute-start.39 = (bf16[1024,256]{1,0:T(8,128)(2,1)S(1)}, bf16[1024,256]{1,0:T(8,128)(2,1)S(1)}, u32[]{:S(2)}, u32[]{:S(2)}) collective-permute-start(bf16[1024,256]{1,0:T(8,128)(2,1)S(1)} %add_convert_fusion.67), channel_id=1, source_target_pairs={{0,6},{1,7},{2,0},{3,1},{4,2},{5,3},{6,4},{7,5},{8,14},{9,15},{10,... | collective-permute-start | bytes 1572872 | tf_op jit(solution)/shard_map/ppermute | solution.py:78
  625.4 19.6 %collective-permute-start.43 = (bf16[1024,256]{1,0:T(8,128)(2,1)S(1)}, bf16[1024,256]{1,0:T(8,128)(2,1)S(1)}, u32[]{:S(2)}, u32[]{:S(2)}) collective-permute-start(bf16[1024,256]{1,0:T(8,128)(2,1)S(1)} %add_convert_fusion.66), channel_id=1, source_target_pairs={{0,6},{1,7},{2,0},{3,1},{4,2},{5,3},{6,4},{7,5},{8,14},{9,15},{10,... | collective-permute-start | bytes 1572872 | tf_op jit(solution)/shard_map/ppermute | solution.py:78
  677.4 19.6 %collective-permute-start.47 = (bf16[1024,256]{1,0:T(8,128)(2,1)S(1)}, bf16[1024,256]{1,0:T(8,128)(2,1)S(1)}, u32[]{:S(2)}, u32[]{:S(2)}) collective-permute-start(bf16[1024,256]{1,0:T(8,128)(2,1)S(1)} %add_convert_fusion.65), channel_id=1, source_target_pairs={{0,6},{1,7},{2,0},{3,1},{4,2},{5,3},{6,4},{7,5},{8,14},{9,15},{10,... | collective-permute-start | bytes 1572872 | tf_op jit(solution)/shard_map/ppermute | solution.py:78
  680.7 17.1 collective-permute-start.48
  729.4 19.6 %collective-permute-start.51 = (bf16[1024,256]{1,0:T(8,128)(2,1)S(1)}, bf16[1024,256]{1,0:T(8,128)(2,1)S(1)}, u32[]{:S(2)}, u32[]{:S(2)}) collective-permute-start(bf16[1024,256]{1,0:T(8,128)(2,1)S(1)} %add_convert_fusion.64), channel_id=1, source_target_pairs={{0,6},{1,7},{2,0},{3,1},{4,2},{5,3},{6,4},{7,5},{8,14},{9,15},{10,... | collective-permute-start | bytes 1572872 | tf_op jit(solution)/shard_map/ppermute | solution.py:78
  781.5 19.6 %collective-permute-start.55 = (bf16[1024,256]{1,0:T(8,128)(2,1)S(1)}, bf16[1024,256]{1,0:T(8,128)(2,1)S(1)}, u32[]{:S(2)}, u32[]{:S(2)}) collective-permute-start(bf16[1024,256]{1,0:T(8,128)(2,1)S(1)} %add_convert_fusion.63), channel_id=1, source_target_pairs={{0,6},{1,7},{2,0},{3,1},{4,2},{5,3},{6,4},{7,5},{8,14},{9,15},{10,... | collective-permute-start | bytes 1572872 | tf_op jit(solution)/shard_map/ppermute | solution.py:78
  833.8 19.6 %collective-permute-start.59 = (bf16[1024,256]{1,0:T(8,128)(2,1)S(1)}, bf16[1024,256]{1,0:T(8,128)(2,1)S(1)}, u32[]{:S(2)}, u32[]{:S(2)}) collective-permute-start(bf16[1024,256]{1,0:T(8,128)(2,1)S(1)} %add_convert_fusion.62), channel_id=1, source_target_pairs={{0,6},{1,7},{2,0},{3,1},{4,2},{5,3},{6,4},{7,5},{8,14},{9,15},{10,... | collective-permute-start | bytes 1572872 | tf_op jit(solution)/shard_map/ppermute | solution.py:78
  885.7 19.6 %collective-permute-start.63 = (bf16[1024,256]{1,0:T(8,128)(2,1)S(1)}, bf16[1024,256]{1,0:T(8,128)(2,1)S(1)}, u32[]{:S(2)}, u32[]{:S(2)}) collective-permute-start(bf16[1024,256]{1,0:T(8,128)(2,1)S(1)} %add_convert_fusion.61), channel_id=1, source_target_pairs={{0,6},{1,7},{2,0},{3,1},{4,2},{5,3},{6,4},{7,5},{8,14},{9,15},{10,... | collective-permute-start | bytes 1572872 | tf_op jit(solution)/shard_map/ppermute | solution.py:78
  1039.8 17.2 collective-permute-start.69
  1071.1 20.4 %collective-permute-start.73 = (bf16[1024,256]{1,0:T(8,128)(2,1)S(1)}, bf16[1024,256]{1,0:T(8,128)(2,1)S(1)}, u32[]{:S(2)}, u32[]{:S(2)}) collective-permute-start(bf16[1024,256]{1,0:T(8,128)(2,1)S(1)} %add_convert_fusion.59), channel_id=1, source_target_pairs={{0,6},{1,7},{2,0},{3,1},{4,2},{5,3},{6,4},{7,5},{8,14},{9,15},{10,... | collective-permute-start | bytes 1572872 | tf_op jit(solution)/shard_map/ppermute | solution.py:78
  1074.8 17.5 collective-permute-start.74
  1124.1 19.2 %collective-permute-start.77 = (bf16[1024,256]{1,0:T(8,128)(2,1)S(1)}, bf16[1024,256]{1,0:T(8,128)(2,1)S(1)}, u32[]{:S(2)}, u32[]{:S(2)}) collective-permute-start(bf16[1024,256]{1,0:T(8,128)(2,1)S(1)} %add_convert_fusion.58), channel_id=1, source_target_pairs={{0,6},{1,7},{2,0},{3,1},{4,2},{5,3},{6,4},{7,5},{8,14},{9,15},{10,... | collective-permute-start | bytes 1572872 | tf_op jit(solution)/shard_map/ppermute | solution.py:78
  1127.1 17.1 collective-permute-start.78
  1176.2 19.6 %collective-permute-start.81 = (bf16[1024,256]{1,0:T(8,128)(2,1)S(1)}, bf16[1024,256]{1,0:T(8,128)(2,1)S(1)}, u32[]{:S(2)}, u32[]{:S(2)}) collective-permute-start(bf16[1024,256]{1,0:T(8,128)(2,1)S(1)} %add_convert_fusion.57), channel_id=1, source_target_pairs={{0,6},{1,7},{2,0},{3,1},{4,2},{5,3},{6,4},{7,5},{8,14},{9,15},{10,... | collective-permute-start | bytes 1572872 | tf_op jit(solution)/shard_map/ppermute | solution.py:78
  1228.2 19.6 %collective-permute-start.85 = (bf16[1024,256]{1,0:T(8,128)(2,1)S(1)}, bf16[1024,256]{1,0:T(8,128)(2,1)S(1)}, u32[]{:S(2)}, u32[]{:S(2)}) collective-permute-start(bf16[1024,256]{1,0:T(8,128)(2,1)S(1)} %add_convert_fusion.56), channel_id=1, source_target_pairs={{0,6},{1,7},{2,0},{3,1},{4,2},{5,3},{6,4},{7,5},{8,14},{9,15},{10,... | collective-permute-start | bytes 1572872 | tf_op jit(solution)/shard_map/ppermute | solution.py:78
  1231.5 17.1 collective-permute-start.86
  1280.4 19.6 %collective-permute-start.89 = (bf16[1024,256]{1,0:T(8,128)(2,1)S(1)}, bf16[1024,256]{1,0:T(8,128)(2,1)S(1)}, u32[]{:S(2)}, u32[]{:S(2)}) collective-permute-start(bf16[1024,256]{1,0:T(8,128)(2,1)S(1)} %add_convert_fusion.55), channel_id=1, source_target_pairs={{0,6},{1,7},{2,0},{3,1},{4,2},{5,3},{6,4},{7,5},{8,14},{9,15},{10,... | collective-permute-start | bytes 1572872 | tf_op jit(solution)/shard_map/ppermute | solution.py:78
  1283.7 17.1 collective-permute-start.90
  1332.7 19.6 %collective-permute-start.93 = (bf16[1024,256]{1,0:T(8,128)(2,1)S(1)}, bf16[1024,256]{1,0:T(8,128)(2,1)S(1)}, u32[]{:S(2)}, u32[]{:S(2)}) collective-permute-start(bf16[1024,256]{1,0:T(8,128)(2,1)S(1)} %add_convert_fusion.54), channel_id=1, source_target_pairs={{0,6},{1,7},{2,0},{3,1},{4,2},{5,3},{6,4},{7,5},{8,14},{9,15},{10,... | collective-permute-start | bytes 1572872 | tf_op jit(solution)/shard_map/ppermute | solution.py:78
  1385.1 19.6 %collective-permute-start.97 = (bf16[1024,256]{1,0:T(8,128)(2,1)S(1)}, bf16[1024,256]{1,0:T(8,128)(2,1)S(1)}, u32[]{:S(2)}, u32[]{:S(2)}) collective-permute-start(bf16[1024,256]{1,0:T(8,128)(2,1)S(1)} %add_convert_fusion.53), channel_id=1, source_target_pairs={{0,6},{1,7},{2,0},{3,1},{4,2},{5,3},{6,4},{7,5},{8,14},{9,15},{10,... | collective-permute-start | bytes 1572872 | tf_op jit(solution)/shard_map/ppermute | solution.py:78
  1388.4 17.1 collective-permute-start.98
  1437.1 19.6 %collective-permute-start.101 = (bf16[1024,256]{1,0:T(8,128)(2,1)S(1)}, bf16[1024,256]{1,0:T(8,128)(2,1)S(1)}, u32[]{:S(2)}, u32[]{:S(2)}) collective-permute-start(bf16[1024,256]{1,0:T(8,128)(2,1)S(1)} %add_convert_fusion.52), channel_id=1, source_target_pairs={{0,6},{1,7},{2,0},{3,1},{4,2},{5,3},{6,4},{7,5},{8,14},{9,15},{10,... | collective-permute-start | bytes 1572872 | tf_op jit(solution)/shard_map/ppermute | solution.py:78
  1440.4 17.1 collective-permute-start.102
  1489.3 19.6 %collective-permute-start.105 = (bf16[1024,256]{1,0:T(8,128)(2,1)S(1)}, bf16[1024,256]{1,0:T(8,128)(2,1)S(1)}, u32[]{:S(2)}, u32[]{:S(2)}) collective-permute-start(bf16[1024,256]{1,0:T(8,128)(2,1)S(1)} %add_convert_fusion.51), channel_id=1, source_target_pairs={{0,6},{1,7},{2,0},{3,1},{4,2},{5,3},{6,4},{7,5},{8,14},{9,15},{10,... | collective-permute-start | bytes 1572872 | tf_op jit(solution)/shard_map/ppermute | solution.py:78
  1492.6 17.1 collective-permute-start.106
  1541.6 19.6 %collective-permute-start.109 = (bf16[1024,256]{1,0:T(8,128)(2,1)S(1)}, bf16[1024,256]{1,0:T(8,128)(2,1)S(1)}, u32[]{:S(2)}, u32[]{:S(2)}) collective-permute-start(bf16[1024,256]{1,0:T(8,128)(2,1)S(1)} %add_convert_fusion.50), channel_id=1, source_target_pairs={{0,6},{1,7},{2,0},{3,1},{4,2},{5,3},{6,4},{7,5},{8,14},{9,15},{10,... | collective-permute-start | bytes 1572872 | tf_op jit(solution)/shard_map/ppermute | solution.py:78
  1544.9 17.1 collective-permute-start.110
  1594.0 19.6 %collective-permute-start.113 = (bf16[1024,256]{1,0:T(8,128)(2,1)S(1)}, bf16[1024,256]{1,0:T(8,128)(2,1)S(1)}, u32[]{:S(2)}, u32[]{:S(2)}) collective-permute-start(bf16[1024,256]{1,0:T(8,128)(2,1)S(1)} %add_convert_fusion.49), channel_id=1, source_target_pairs={{0,6},{1,7},{2,0},{3,1},{4,2},{5,3},{6,4},{7,5},{8,14},{9,15},{10,... | collective-permute-start | bytes 1572872 | tf_op jit(solution)/shard_map/ppermute | solution.py:78
  1646.0 19.6 %collective-permute-start.117 = (bf16[1024,256]{1,0:T(8,128)(2,1)S(1)}, bf16[1024,256]{1,0:T(8,128)(2,1)S(1)}, u32[]{:S(2)}, u32[]{:S(2)}) collective-permute-start(bf16[1024,256]{1,0:T(8,128)(2,1)S(1)} %add_convert_fusion.48), channel_id=1, source_target_pairs={{0,6},{1,7},{2,0},{3,1},{4,2},{5,3},{6,4},{7,5},{8,14},{9,15},{10,... | collective-permute-start | bytes 1572872 | tf_op jit(solution)/shard_map/ppermute | solution.py:78
  1649.3 17.1 collective-permute-start.118
  1698.2 19.6 %collective-permute-start.121 = (bf16[1024,256]{1,0:T(8,128)(2,1)S(1)}, bf16[1024,256]{1,0:T(8,128)(2,1)S(1)}, u32[]{:S(2)}, u32[]{:S(2)}) collective-permute-start(bf16[1024,256]{1,0:T(8,128)(2,1)S(1)} %add_convert_fusion.47), channel_id=1, source_target_pairs={{0,6},{1,7},{2,0},{3,1},{4,2},{5,3},{6,4},{7,5},{8,14},{9,15},{10,... | collective-permute-start | bytes 1572872 | tf_op jit(solution)/shard_map/ppermute | solution.py:78
  1701.5 17.1 collective-permute-start.122
  1750.5 19.6 %collective-permute-start.125 = (bf16[1024,256]{1,0:T(8,128)(2,1)S(1)}, bf16[1024,256]{1,0:T(8,128)(2,1)S(1)}, u32[]{:S(2)}, u32[]{:S(2)}) collective-permute-start(bf16[1024,256]{1,0:T(8,128)(2,1)S(1)} %add_convert_fusion.46), channel_id=1, source_target_pairs={{0,6},{1,7},{2,0},{3,1},{4,2},{5,3},{6,4},{7,5},{8,14},{9,15},{10,... | collective-permute-start | bytes 1572872 | tf_op jit(solution)/shard_map/ppermute | solution.py:78
  1753.8 17.1 collective-permute-start.126
  1802.5 19.6 %collective-permute-start.129 = (bf16[1024,256]{1,0:T(8,128)(2,1)S(1)}, bf16[1024,256]{1,0:T(8,128)(2,1)S(1)}, u32[]{:S(2)}, u32[]{:S(2)}) collective-permute-start(bf16[1024,256]{1,0:T(8,128)(2,1)S(1)} %add_convert_fusion.45), channel_id=1, source_target_pairs={{0,6},{1,7},{2,0},{3,1},{4,2},{5,3},{6,4},{7,5},{8,14},{9,15},{10,... | collective-permute-start | bytes 1572872 | tf_op jit(solution)/shard_map/ppermute | solution.py:78
  1805.8 17.1 collective-permute-start.130
  (171 other events, 3117.1 us)
where the time goes:
time: 1920 us; the launch traced here: 1900 us
  matrix products  643 us (33%)
  other arithmetic  400 us (21%)
  local copies, waits for them, and re-layouts  365 us (19%)
  waiting for transfers between devices  274 us (14%)
  starting transfers between devices  216 us (11%)
    dot_general x186, matrix products, matmul_f32(): return jnp.dot(values, weight, preferred_element_type=jnp.float32)  639 us
    ppermute x32, waiting for transfers between devices, local_run(): lax.ppermute(mesh_cur[mesh_dev - half_shard:], 'gp', shift_pairs(1))  270 us
    unnamed x463, local copies, waits for them, and re-layouts  267 us
    reduce_sum x32, other arithmetic, local_run(): edge_sum = jnp.sum(edge_lat, axis=1, dtype=jnp.float32).astype(jnp.bfloat16)  182 us
    reduce_sum x80, other arithmetic, layer_norm(): spread = jnp.mean(centred * centred, axis=-1, keepdims=True)  169 us
    ppermute x32, starting transfers between devices, local_run(): far_plus = lax.ppermute(mesh_cur, 'gp', shift_pairs(-quarter_hop))  102 us
    ppermute x32, starting transfers between devices, local_run(): lax.ppermute(mesh_cur[mesh_dev - half_shard:], 'gp', shift_pairs(1))  87.4 us
  transfers between devices with their start and end apart: 132, of which 33 were waited for; matrix products, arithmetic and copies ran while one was open for 13% of the time, Pallas kernels for 0%

commit v1 on v0

v1 whole, which is shorter than its diff:
```python
import jax
import jax.numpy as jnp
import numpy as np
from jax import lax
from jax.experimental import pallas as pl
from jax.experimental.pallas import tpu as pltpu
from jax.sharding import PartitionSpec as P

MESH_ID = pl.DeviceIdType.MESH
F32 = jnp.float32
BF16 = jnp.bfloat16
SUB = 256


def dot(a, b):
    return jnp.dot(a, b, preferred_element_type=F32)


def silu(x):
    half = 0.5 * x
    return (half * jnp.tanh(half) + half).astype(BF16)


def norm(y):
    z = y - jnp.mean(y, axis=-1, keepdims=True)
    return z * lax.rsqrt(jnp.mean(z * z, axis=-1, keepdims=True) + 1e-5)


def residual(base, update):
    return (base.astype(F32) + update).astype(BF16)


def row_permutation():
    perm = np.zeros((256, 256), np.float32)
    for r in range(4):
        for j in range(8):
            for i in range(8):
                perm[r * 64 + j * 8 + i, (i * 8 + j) * 4 + r] = 1.0
    return np.stack([perm, perm.T])


def solution(mesh):
    group = mesh.shape["gp"]

    def kernel(f0, xc_hbm, ef_hbm, mf, stats, perms, wg, wemb, wembo, wei_hbm, weo_hbm, wni_hbm, wno_hbm, wgs, woh, wof,
               out0, out1,
               wei, weo, wni, wno, xst, xs, fm, g2m, m2g, glat, gcur, mlat, efl, ebase, elat, hsend, hin, hcur, hd,
               proj, recv, halo_s, halo_r, stage,
               wsem, xsem, osem, ef_s, ef_r, en_s, en_r, de_s, de_r, ha_s, ha_r):
        me = lax.axis_index("gp")
        left = lax.rem(me + group - 1, group)
        right = lax.rem(me + 1, group)
        blocks = 2 * group
        layers = wei_hbm.shape[0]

        barrier = pltpu.get_barrier_semaphore()
        for hop in range(1, group):
            pl.semaphore_signal(barrier, inc=1, device_id={"gp": lax.rem(me + hop, group)}, device_id_type=MESH_ID)

        weight_copies = [pltpu.make_async_copy(src, dst, wsem.at[i]) for i, (src, dst) in enumerate(
            [(wei_hbm, wei), (weo_hbm, weo), (wni_hbm, wni), (wno_hbm, wno)])]
        x_copy = pltpu.make_async_copy(xc_hbm, xst.at[0], xsem)
        x_copy.start()
        for copy in weight_copies:
            copy.start()
        pl.semaphore_wait(barrier, group - 1)

        def block_of(device, half):
            return lax.rem(2 * device + half, blocks)

        def ef_copy(hop, half):
            dest = lax.rem(me + hop, group)
            return pltpu.make_async_remote_copy(
                src_ref=ef_hbm.at[half, dest], dst_ref=efl.at[2 * me + half], send_sem=ef_s.at[dest, half],
                recv_sem=ef_r.at[me, half], device_id={"gp": dest}, device_id_type=MESH_ID)

        def ef_keep(half):
            return pltpu.make_async_copy(ef_hbm.at[half, me], efl.at[2 * me + half], ef_r.at[me, half])

        for half in range(2):
            for hop in range(1, group):
                ef_copy(hop, half).start()
            ef_keep(half).start()

        def embed_rows(it, carry):
            for sub in range(4):
                base = pl.multiple_of((it * 4 + sub) * 256, 256)
                rows = pl.ds(base, 256)
                feats = dot(perms[0], f0[rows, :]).astype(BF16)
                xs[0, rows, :] = feats[:, 0:128]
                xs[1, rows, :] = feats[:, 128:256]
                misc = feats[:, 256:384]
                fm[rows, :] = misc
                g2m[rows, :] = norm(dot(silu(dot(misc, wemb[0])), wembo[2])).astype(BF16)
                m2g[rows, :] = norm(dot(silu(dot(misc, wemb[1])), wembo[3])).astype(BF16)
            return carry

        lax.fori_loop(0, 4, embed_rows, 0)
        for sub in range(4):
            rows = pl.ds(sub * 256, 256)
            mlat[rows, :] = norm(dot(silu(dot(mf[rows, :], wemb[2])), wembo[1])).astype(BF16)
        xs[2] = jnp.zeros(xs.shape[1:], BF16)
        for copy in weight_copies:
            copy.wait()

        def en_copy(hop, half):
            dest = lax.rem(me + hop, group)
            return pltpu.make_async_remote_copy(
                src_ref=hsend.at[half, dest], dst_ref=hin.at[block_of(me, 1 + half)], send_sem=en_s.at[dest, half],
                recv_sem=en_r.at[me, half], device_id={"gp": dest}, device_id_type=MESH_ID)

        def de_copy(hop, half):
            dest = lax.rem(me + hop, group)
            return pltpu.make_async_remote_copy(
                src_ref=hcur.at[block_of(dest, 1 + half)], dst_ref=hd.at[half, me], send_sem=de_s.at[dest, half],
                recv_sem=de_r.at[me, half], device_id={"gp": dest}, device_id_type=MESH_ID)

        def en_arrival(source, half):
            return pltpu.make_async_remote_copy(
                src_ref=hsend.at[half, me], dst_ref=hin.at[block_of(source, 1 + half)], send_sem=en_s.at[me, half],
                recv_sem=en_r.at[source, half], device_id={"gp": left}, device_id_type=MESH_ID)

        def de_arrival(source, half):
            return pltpu.make_async_remote_copy(
                src_ref=hcur.at[0], dst_ref=hd.at[half, source], send_sem=de_s.at[me, half],
                recv_sem=de_r.at[source, half], device_id={"gp": left}, device_id_type=MESH_ID)

        def ef_arrival(source, half):
            return pltpu.make_async_remote_copy(
                src_ref=ef_hbm.at[half, me], dst_ref=efl.at[2 * source + half], send_sem=ef_s.at[me, half],
                recv_sem=ef_r.at[source, half], device_id={"gp": left}, device_id_type=MESH_ID)

        def halo_copies(slot):
            return [pltpu.make_async_remote_copy(
                src_ref=halo_s.at[slot, side], dst_ref=halo_r.at[slot, 1 - side], send_sem=ha_s.at[slot, side],
                recv_sem=ha_r.at[slot, 1 - side], device_id={"gp": (left, right)[side]}, device_id_type=MESH_ID)
                for side in range(2)]

        def send_halo(slot):
            for b in range(blocks):
                stage[0, b:b + 1, :] = hcur[b, 0:16, :].astype(F32)[0:1]
                stage[1, b:b + 1, :] = hcur[b, 48:64, :].astype(F32)[15:16]
            halo_s[slot, 0] = stage[0].astype(BF16)
            halo_s[slot, 1] = stage[1].astype(BF16)
            for copy in halo_copies(slot):
                copy.start()

        def rolled(shift):
            cut = shift % blocks
            return jnp.concatenate([proj[cut:, 8:72, :], proj[:cut, 8:72, :]], axis=0)

        def edge_update(layer, k, send):
            send = send.reshape(blocks * 64, 256)
            w_first = wei[layer, 0:256, :]
            w_second = weo[layer]
            for sub in range(0, blocks * 64, SUB):
                rows = slice(sub, sub + SUB)
                old = elat[k, rows, :]
                pre = dot(old, w_first) + (send[rows] + recv[rows, :])
                elat[k, rows, :] = residual(old, norm(dot(silu(pre), w_second)))

        def mesh_layer(layer, carry):
            slot = lax.rem(layer, 2)
            h = hcur[...].reshape(blocks * 64, 256)
            proj[:, 8:72, :] = dot(h, wei[layer, 256:512, :]).reshape(blocks, 64, 256)
            recv[...] = dot(h, wei[layer, 512:768, :])
            for k, shift in ((2, 1), (3, -1), (4, 4), (5, -4)):
                edge_update(layer, k, rolled(shift))
            for copy in halo_copies(slot):
                copy.wait_recv()
            for copy in halo_copies(slot):
                copy.wait_send()
            edge_proj = dot(halo_r[slot].reshape(32, 256), wei[layer, 256:512, :])
            low = edge_proj[0:16]
            high = edge_proj[16:32]
            stage[0] = jnp.where(me == 0, jnp.concatenate([low[15:16], low[0:15]], axis=0), low)
            stage[1] = jnp.where(me == group - 1, jnp.concatenate([high[1:16], high[0:1]], axis=0), high)
            sublane = lax.broadcasted_iota(jnp.int32, (8, 256), 0)
            for b in range(blocks):
                proj[b, 0:8, :] = jnp.where(sublane == 0, stage[0, b:b + 1, :], pltpu.roll(proj[b, 64:72, :], 1, 0))
                proj[b, 72:80, :] = jnp.where(sublane == 7, stage[1, b:b + 1, :], pltpu.roll(proj[b, 8:16, :], 7, 0))
            edge_update(layer, 0, proj[:, 16:80, :])
            edge_update(layer, 1, proj[:, 0:64, :])
            for sub in range(0, blocks, SUB // 64):
                node = hcur[sub:sub + SUB // 64].reshape(SUB, 256)
                rows = slice(sub * 64, sub * 64 + SUB)
                total = elat[0, rows, :].astype(F32)
                for k in range(1, 6):
                    total = total + elat[k, rows, :].astype(F32)
                pre = dot(node, wni[layer, 0:256, :]) + dot(total.astype(BF16), wni[layer, 256:512, :])
                new = residual(node, norm(dot(silu(pre), wno[layer])))
                hcur[sub:sub + SUB // 64] = new.reshape(SUB // 64, 64, 256)

            @pl.when(layer < layers - 2)
            def _():
                send_halo(1 - slot)
            return carry

        def forecast(step, carry):
            def encode(it, carry):
                for q in range(2):
                    hop = 2 * it + 1 + q
                    dest = lax.rem(me + hop, group)
                    esums = []
                    nodes = []
                    for half in range(2):
                        chunk = half * group + dest
                        rows = pl.ds(pl.multiple_of(chunk * 256, 256), 256)
                        mrows = pl.ds(pl.multiple_of(chunk * 64, 64), 64)
                        feats = jnp.concatenate([xs[step, rows, :], xs[step + 1, rows, :]], axis=1)
                        pre = dot(feats, wg[step, 0:256, :]) + dot(fm[rows, :], wg[step, 256:384, :])
                        lat = norm(dot(silu(pre), wembo[0])).astype(BF16)
                        glat[rows, :] = lat
                        node = mlat[mrows, :]
                        term = dot(node, wei[0, 512:768, :])
                        old = g2m[rows, :]
                        pre = dot(old, wei[0, 0:256, :]) + dot(lat, wei[0, 256:512, :])
                        pre = pre + jnp.concatenate([term] * 4, axis=0)
                        edge = residual(old, norm(dot(silu(pre), weo[0]))).astype(F32)
                        esums.append((edge[0:64] + edge[64:128] + edge[128:192] + edge[192:256]).astype(BF16))
                        nodes.append(node)
                    node = jnp.concatenate(nodes, axis=0)
                    pre = dot(node, wni[0, 0:256, :]) + dot(jnp.concatenate(esums, axis=0), wni[0, 256:512, :])
                    new = residual(node, norm(dot(silu(pre), wno[0])))
                    for half in range(2):
                        hsend[half, dest] = new[half * 64:half * 64 + 64]
                for half in range(2):
                    en_copy(2 * it + 1, half).start()

                @pl.when(it < group // 2 - 1)
                def _():
                    for half in range(2):
                        en_copy(2 * it + 2, half).start()
                return carry

            lax.fori_loop(0, group // 2, encode, 0)

            @pl.when(step == 0)
            def _():
                for half in range(2):
                    for hop in range(1, group):
                        ef_arrival(lax.rem(me + hop, group), half).wait_recv()
                    ef_keep(half).wait()

                def embed_edges(k, carry):
                    for sub in range(0, blocks, 4):
                        feats = efl[sub:sub + 4].reshape(256, 128)
                        ebase[k, sub * 64:sub * 64 + 256, :] = norm(dot(silu(dot(feats, wemb[3 + k])), wembo[4])).astype(BF16)
                    return carry

                lax.fori_loop(0, 6, embed_edges, 0)
                for hop in range(1, group):
                    for half in range(2):
                        ef_copy(hop, half).wait_send()

            elat[...] = ebase[...]
            for hop in range(1, group):
                for half in range(2):
                    en_arrival(lax.rem(me + hop, group), half).wait_recv()
            for hop in range(1, group):
                for half in range(2):
                    en_copy(hop, half).wait_send()
            hcur[...] = hin[...]
            for half in range(2):
                hcur[block_of(me, 1 + half)] = hsend[half, me]
            send_halo(1)
            lax.fori_loop(1, layers - 1, mesh_layer, 0)
            for hop in range(1, group):
                for half in range(2):
                    de_copy(hop, half).start()
            for half in range(2):
                hd[half, me] = hcur[block_of(me, 1 + half)]

            def self_update(it, carry):
                for sub in range(4):
                    rows = pl.ds(pl.multiple_of((it * 4 + sub) * 256, 256), 256)
                    old = glat[rows, :]
                    gcur[rows, :] = residual(old, norm(dot(silu(dot(old, wgs[0])), wgs[1])))
                return carry

            lax.fori_loop(0, 4, self_update, 0)

            @pl.when(step == 0)
            def _():
                x_copy.wait()

            def decode(it, carry):
                last = layers - 1
                for half in range(2):
                    de_arrival(lax.rem(me + 2 * it + 1, group), half).wait_recv()

                @pl.when(it < group // 2 - 1)
                def _():
                    for half in range(2):
                        de_arrival(lax.rem(me + 2 * it + 2, group), half).wait_recv()

                work = []
                for q in range(2):
                    source = lax.rem(me + 2 * it + 1 + q, group)
                    for half in range(2):
                        rows = pl.ds(pl.multiple_of((half * group + source) * 256, 256), 256)
                        work.append((rows, hd[half, source], m2g[rows, :], gcur[rows, :], xst[step, rows, :]))
                done = []
                for rows, node, old, grid, state in work:
                    term = dot(node, wei[last, 256:512, :])
                    pre = dot(old, wei[last, 0:256, :]) + dot(grid, wei[last, 512:768, :])
                    pre = pre + jnp.concatenate([term] * 4, axis=0)
                    edge = residual(old, norm(dot(silu(pre), weo[last])))
                    pre = dot(grid, wni[last, 0:256, :]) + dot(edge, wni[last, 256:512, :])
                    out = residual(grid, norm(dot(silu(pre), wno[last])))
                    hidden = silu(dot(out, woh[...]))
                    hidden = dot(perms[1], hidden).astype(BF16)
                    new = state + stats[3:4, :] * dot(hidden, wof[...]) + stats[2:3, :]
                    scaled = ((new - stats[0:1, :]) / stats[1:2, :]).astype(BF16)
                    done.append((rows, new, dot(perms[0], scaled).astype(BF16)))
                for rows, new, scaled in done:
                    xst[step + 1, rows, :] = new
                    xs[2, rows, 0:scaled.shape[1]] = scaled
                return carry

            lax.fori_loop(0, group // 2, decode, 0)
            for hop in range(1, group):
                for half in range(2):
                    de_copy(hop, half).wait_send()

            @pl.when(step == 0)
            def _():
                pltpu.make_async_copy(xst.at[1], out0, osem.at[0]).start()
            return carry

        lax.fori_loop(0, 2, forecast, 0)
        final = pltpu.make_async_copy(xst.at[2], out1, osem.at[1])
        final.start()
        pltpu.make_async_copy(xst.at[1], out0, osem.at[0]).wait()
        final.wait()

    def shift_pairs(hop_count):
        return [(source, (source + hop_count) % group) for source in range(group)]

    def local_run(x_prev, x_cur, forcing, grid_static, g2m_feat, m2g_feat, mesh_feat, mesh_edge_feat, norm_stats, w_grid_in, w_mesh_in, w_eemb_in, w_embed_out, w_edge_in, w_edge_out, w_node_in, w_node_out, w_grid_self, w_out_hidden, w_out_final):
        grid_dev, variables = x_prev.shape
        mesh_dev = mesh_feat.shape[0]
        latent = w_embed_out.shape[-1]
        blocks = 2 * group
        half_grid = grid_dev // 2
        half_mesh = mesh_dev // 2

        def shifted(values, half):
            head = lax.ppermute(values[:half], "gp", shift_pairs(-1))
            return jnp.concatenate([values[half:], head], axis=0)

        def in_order(values):
            lanes = values.shape[-1]
            values = values.reshape(2, group, 8, 8, lanes).transpose(0, 1, 3, 2, 4)
            return values.reshape(2, group, 64, lanes)

        def lane_pad(values, width):
            return jnp.pad(values, [(0, 0)] * (values.ndim - 1) + [(0, width - values.shape[-1])])

        g2m_here = shifted(g2m_feat, half_grid)
        mesh_here = shifted(mesh_feat, half_mesh)
        misc = jnp.concatenate([forcing[:, 0, :], forcing[:, 1, :], grid_static, g2m_here, m2g_feat], axis=1)
        force = forcing.shape[-1]
        static = grid_static.shape[-1]
        edge_lanes = g2m_feat.shape[-1]
        scale = lambda x: (x - norm_stats[0]) / norm_stats[1]
        feats = jnp.concatenate([lane_pad(scale(x_prev), 128), lane_pad(scale(x_cur), 128), lane_pad(misc, 128)], axis=1).astype(BF16)
        mesh_rows = lane_pad(in_order(mesh_here).astype(BF16), 128).reshape(mesh_dev, 128)
        edge_rows = lane_pad(in_order(mesh_edge_feat.reshape(mesh_dev, -1)).astype(BF16), 128)

        def placed(rows, start, height):
            return jnp.pad(rows, ((start, height - start - rows.shape[0]), (0, 0)))

        w_force = w_grid_in[2 * variables:2 * variables + force]
        w_static = w_grid_in[2 * variables + force:]
        w_state = placed(w_grid_in[:variables], 0, 384) + placed(w_grid_in[variables:2 * variables], 128, 384) + placed(w_static, 256 + 2 * force, 384)
        w_grid = jnp.stack([w_state + placed(w_force, 256 + force * s, 384) for s in range(2)])
        at_g2m = 2 * force + static
        w_embed = jnp.stack([placed(w_eemb_in[0], at_g2m, 128), placed(w_eemb_in[1], at_g2m + edge_lanes, 128), placed(w_mesh_in, 0, 128)]
                            + [placed(w_eemb_in[2], edge_lanes * k, 128) for k in range(6)])
        perms = jnp.asarray(row_permutation(), BF16)

        vmem = pl.BlockSpec(memory_space=pltpu.VMEM)
        anywhere = pl.BlockSpec(memory_space=pl.ANY)
        state = jax.ShapeDtypeStruct((grid_dev, variables), F32)
        dma = pltpu.SemaphoreType.DMA
        return pl.pallas_call(
            kernel,
            out_shape=(state, state),
            in_specs=[vmem, anywhere, anywhere] + [vmem] * 6 + [anywhere] * 4 + [vmem] * 3,
            out_specs=(anywhere, anywhere),
            scratch_shapes=[
                pltpu.VMEM(w_edge_in.shape, BF16), pltpu.VMEM(w_edge_out.shape, BF16),
                pltpu.VMEM(w_node_in.shape, BF16), pltpu.VMEM(w_node_out.shape, BF16),
                pltpu.VMEM((3, grid_dev, variables), F32), pltpu.VMEM((3, grid_dev, 128), BF16), pltpu.VMEM((grid_dev, 128), BF16),
                pltpu.VMEM((grid_dev, latent), BF16), pltpu.VMEM((grid_dev, latent), BF16), pltpu.VMEM((grid_dev, latent), BF16),
                pltpu.VMEM((grid_dev, latent), BF16),
                pltpu.VMEM((mesh_dev, latent), BF16), pltpu.VMEM((blocks, 64, 128), BF16),
                pltpu.VMEM((6, mesh_dev, latent), BF16), pltpu.VMEM((6, mesh_dev, latent), BF16),
                pltpu.VMEM((2, group, 64, latent), BF16), pltpu.VMEM((blocks, 64, latent), BF16),
                pltpu.VMEM((blocks, 64, latent), BF16), pltpu.VMEM((2, group, 64, latent), BF16),
                pltpu.VMEM((blocks, 80, latent), F32), pltpu.VMEM((mesh_dev, latent), F32),
                pltpu.VMEM((2, 2, blocks, latent), BF16), pltpu.VMEM((2, 2, blocks, latent), BF16), pltpu.VMEM((2, blocks, latent), F32),
                dma((4,)), dma, dma((2,)), dma((group, 2)), dma((group, 2)), dma((group, 2)), dma((group, 2)),
                dma((group, 2)), dma((group, 2)), dma((2, 2)), dma((2, 2)),
            ],
            compiler_params=pltpu.CompilerParams(collective_id=0, has_side_effects=True, vmem_limit_bytes=67043328),
        )(feats, x_cur, edge_rows, mesh_rows, norm_stats, perms, w_grid, w_embed, w_embed_out, w_edge_in, w_edge_out, w_node_in, w_node_out,
          w_grid_self, w_out_hidden, w_out_final)

    row_spec = P(("dp", "gp"))
    edge_spec = P(("dp", "gp"), None, None)
    whole = P()
    in_specs = (row_spec, row_spec, edge_spec, row_spec, row_spec, row_spec, row_spec, edge_spec, whole) + (whole,) * 11
    return jax.shard_map(local_run, mesh=mesh, in_specs=in_specs, out_specs=(row_spec, row_spec), check_vma=False)
```

time: 1920 us -> 341 us (0.18)
  matrix products: 643 us -> 0 us
  other arithmetic: 400 us -> 5.98 us
  local copies, waits for them, and re-layouts: 365 us -> 28 us
  Pallas kernels: 0 us -> 302 us
  waiting for transfers between devices: 274 us -> 0.01 us
  starting transfers between devices: 216 us -> 4.15 us
    dot_general x187 -> x0, matrix products: 643 us -> none  [the longest x186 639 us: matmul_f32(): return jnp.dot(values, weight, preferred_element_type=jnp.float32)]
    reduce_sum x114 -> x0, other arithmetic: 359 us -> none  [the longest x32 182 us: local_run(): edge_sum = jnp.sum(edge_lat, axis=1, dtype=jnp.float32).astype(jnp.bfloat16)]
    pallas_call x0 -> x1, Pallas kernels: none -> 302 us  [local_run(): pl.pallas_call(kernel, out_shape=(state, state), in_specs=[vmem, anywhere...]
    ppermute x132 -> x2, waiting for transfers between devices: 274 us -> 0.01 us  [shifted(): head = lax.ppermute(values[:half], 'gp', shift_pairs(-1))]
    unnamed x463 -> x26, local copies, waits for them, and re-layouts: 267 us -> 12.7 us
    ppermute x132 -> x2, starting transfers between devices: 216 us -> 4.15 us  [shifted(): head = lax.ppermute(values[:half], 'gp', shift_pairs(-1))]
    convert_element_type x42 -> x1, other arithmetic: 36 us -> 0.02 us  [local_run(): in_order(mesh_edge_feat.reshape(mesh_dev, -1)).astype(BF16)]
    another operation x32 -> x1, local copies, waits for them, and re-layouts: 31.5 us -> 0.64 us  [local_run(): jnp.stack([placed(w_eemb_in[0], at_g2m, 128), placed(w_eemb_in[1], at_g2m...]
  transfers between devices with their start and end apart: 132 -> 2, of which waited for: 33 -> 0; matrix products, arithmetic and copies ran while one was open for 13% -> 8% of each run, Pallas kernels for 0% -> 0%
where the time goes in v1:
time: 341 us
  Pallas kernels  302 us (89%)
  local copies, waits for them, and re-layouts  28 us (8%)
  other arithmetic  5.98 us (2%)
  starting transfers between devices  4.15 us (1%)
    pallas_call x1, Pallas kernels, local_run(): pl.pallas_call(kernel, out_shape=(state, state), in_specs=[vmem, anywhere...  302 us
    unnamed x26, local copies, waits for them, and re-layouts  12.7 us
  transfers between devices with their start and end apart: 2, of which 0 were waited for; matrix products, arithmetic and copies ran while one was open for 8% of the time, Pallas kernels for 0%

profile of v1, /device:TPU:113, one launch (start us, length us, event | category | flops | bytes accessed | tf_op | source)
XLA Modules:
  0.0 340.6 jit_solution(1358383224714079082)
XLA Ops:
  0.6 0.7 fusion.9
  1.3 0.7 collective-permute-start.1
  2.1 0.8 fusion.8
  2.9 3.4 %collective-permute-start = (bf16[2048,4]{0,1:T(4,128)(2,1)S(1)}, bf16[2048,4]{0,1:T(4,128)(2,1)S(1)}, u32[]{:S(2)}, u32[]{:S(2)}) collective-permute-start(bf16[2048,4]{0,1:T(4,128)(2,1)S(1)} %get-tuple-element.17), channel_id=1, source_target_pairs={{0,7},{1,0},{2,1},{3,2},{4,3},{5,4},{6,5},{7,6},{8,15},{9,8},{10,9... | collective-permute-start | bytes 49160 | tf_op jit(solution)/shard_map/ppermute | solution.py:349
  6.3 0.8 fusion.7
  7.1 0.9 fusion.6
  7.9 0.8 slice_bitcast_fusion.5
  8.7 0.7 slice_bitcast_fusion.2
  9.4 1.0 copy.72
  10.4 0.6 bitcast_dynamic-update-slice_fusion.8
  11.1 0.6 bitcast_dynamic-update-slice_fusion.7
  11.7 1.3 bitcast_dynamic-update-slice_fusion.6
  13.0 0.6 bitcast_dynamic-update-slice_fusion.5
  13.6 0.6 bitcast_dynamic-update-slice_fusion.4
  14.3 0.6 bitcast_dynamic-update-slice_fusion.3
  14.9 0.6 bitcast_dynamic-update-slice_fusion.2
  15.5 0.6 bitcast_dynamic-update-slice_fusion.1
  16.2 1.8 copy.61.xc_hbm
  18.0 0.0 copy-start
  18.0 3.4 copy.59
  21.5 0.8 pad_maximum_fusion.wg
  22.3 0.0 copy-start.4
  22.3 0.0 copy-start.5
  22.3 3.1 divide_convert_fusion.1
  25.3 0.0 copy-done
  25.3 0.6 bitcast_dynamic-update-slice_fusion.wemb
  26.0 0.0 copy-done.4
  26.0 0.0 copy-done.5
  26.0 0.0 copy-done.3
  26.1 0.0 copy-done.6
  26.1 0.7 copy.68.wof
  26.8 0.9 convert_element_type.61
  27.7 0.9 copy.65
  28.6 0.8 pad.81.ef_hbm
  29.4 0.0 collective-permute-done.1
  29.4 0.1 convert_element_type.64
  29.6 0.9 copy.66
  30.4 0.8 pad.82
  31.2 0.0 collective-permute-done
  31.3 0.5 concatenate.17
  31.7 0.5 copy.64
  32.2 0.0 copy-done.1
  32.2 2.0 fusion.5.f0
  34.2 301.7 %shard_map.212 = (f32[4096,78]{1,0:T(8,128)}, f32[4096,78]{1,0:T(8,128)}) custom-call(bf16[4096,384]{1,0:T(8,128)(2,1)} %fusion.5.f0, f32[4096,78]{1,0:T(8,128)} %copy-done, bf16[2,8,64,128]{3,2,1,0:T(8,128)(2,1)} %pad.81.ef_hbm, bf16[1024,128]{1,0:T(8,128)(2,1)} %bitcast.46, f32[4,78]{1,0:T(4,128)} %stats.1, bf16[2,256,256]{2,1,0:T(8,128)(2,1)} %constant.7.clone.perms, ...), custom_call_target="tpu_custom_call" | custom-call | tf_op jit(solution)/shard_map/pallas_call | solution.py:387
  336.0 0.0 copy-start.2
  336.0 2.9 copy.69
  338.9 0.0 copy-done.2
  338.9 1.7 copy.70
  (10 shorter events, 0.1 us)
Async XLA Ops:
  1.3 28.1 %collective-permute-start.1 = (bf16[512,3]{0,1:T(4,128)(2,1)S(1)}, bf16[512,3]{0,1:T(4,128)(2,1)S(1)}, u32[]{:S(2)}, u32[]{:S(2)}) collective-permute-start(bf16[512,3]{0,1:T(4,128)(2,1)S(1)} %get-tuple-element.21), channel_id=1, source_target_pairs={{0,7},{1,0},{2,1},{3,2},{4,3},{5,4},{6,5},{7,6},{8,15},{9,8},{10,9... | collective-permute-start | bytes 9224 | tf_op jit(solution)/shard_map/ppermute | solution.py:349
  2.9 28.4 %collective-permute-start = (bf16[2048,4]{0,1:T(4,128)(2,1)S(1)}, bf16[2048,4]{0,1:T(4,128)(2,1)S(1)}, u32[]{:S(2)}, u32[]{:S(2)}) collective-permute-start(bf16[2048,4]{0,1:T(4,128)(2,1)S(1)} %get-tuple-element.17), channel_id=1, source_target_pairs={{0,7},{1,0},{2,1},{3,2},{4,3},{5,4},{6,5},{7,6},{8,15},{9,8},{10,9... | collective-permute-start | bytes 49160 | tf_op jit(solution)/shard_map/ppermute | solution.py:349
  18.0 7.3 %copy-start = (f32[4096,78]{1,0:T(8,128)}, f32[4096,78]{1,0:T(8,128)S(1)}, u32[]{:S(2)}) copy-start(f32[4096,78]{1,0:T(8,128)S(1)} %copy.61.xc_hbm) | copy-start | bytes 3833860
  22.3 3.7 %copy-start.4 = (f32[4096,3]{0,1:T(4,128)S(1)}, f32[4096,3]{0,1:T(4,128)}, u32[]{:S(2)}) copy-start(f32[4096,3]{0,1:T(4,128)} %param.24) | copy-start | bytes 147460
  22.3 3.7 %copy-start.5 = (f32[4096,4]{0,1:T(4,128)S(1)}, f32[4096,4]{0,1:T(4,128)}, u32[]{:S(2)}) copy-start(f32[4096,4]{0,1:T(4,128)} %param.26) | copy-start | bytes 196612
  22.3 3.8 %copy-start.3 = (f32[1024,6,4]{0,2,1:T(4,128)S(1)}, f32[1024,6,4]{0,2,1:T(4,128)}, u32[]{:S(2)}) copy-start(f32[1024,6,4]{0,2,1:T(4,128)} %param.28) | copy-start | bytes 294916
  22.3 3.8 %copy-start.6 = (bf16[256,78]{0,1:T(8,128)(2,1)S(1)}, bf16[256,78]{0,1:T(8,128)(2,1)}, u32[]{:S(2)}) copy-start(bf16[256,78]{0,1:T(8,128)(2,1)} %param.40) | copy-start | bytes 119812
  26.8 5.4 %copy-start.1 = (bf16[4096,78]{1,0:T(8,128)(2,1)S(1)}, bf16[4096,78]{1,0:T(8,128)(2,1)}, u32[]{:S(2)}) copy-start(bf16[4096,78]{1,0:T(8,128)(2,1)} %get-tuple-element.28) | copy-start | bytes 1916932
  336.0 2.9 copy-start.2

commit v2 on v1

--- a/solution.py
+++ b/solution.py
@@ -10,14 +10,17 @@
 F32 = jnp.float32
 BF16 = jnp.bfloat16
 SUB = 256
+PER = 4
+RECV_MXU = False
+SUM_MXU = False
+FLAGS = {}
 
 
 def dot(a, b):
     return jnp.dot(a, b, preferred_element_type=F32)
 
 
-def silu(x):
-    half = 0.5 * x
+def silu_of_half(half):
     return (half * jnp.tanh(half) + half).astype(BF16)
 
 
@@ -36,7 +39,7 @@
         for j in range(8):
             for i in range(8):
                 perm[r * 64 + j * 8 + i, (i * 8 + j) * 4 + r] = 1.0
-    return np.stack([perm, perm.T])
+    return np.stack([perm, perm.T, np.eye(256, dtype=np.float32)])
 
 
 def solution(mesh):
@@ -45,7 +48,7 @@
     def kernel(f0, xc_hbm, ef_hbm, mf, stats, perms, wg, wemb, wembo, wei_hbm, weo_hbm, wni_hbm, wno_hbm, wgs, woh, wof,
                out0, out1,
                wei, weo, wni, wno, xst, xs, fm, g2m, m2g, glat, gcur, mlat, efl, ebase, elat, hsend, hin, hcur, hd,
-               proj, recv, halo_s, halo_r, stage,
+               proj, recv, halo_s, halo_r, stage, wsh,
                wsem, xsem, osem, ef_s, ef_r, en_s, en_r, de_s, de_r, ha_s, ha_r):
         me = lax.axis_index("gp")
         left = lax.rem(me + group - 1, group)
@@ -91,17 +94,26 @@
                 xs[1, rows, :] = feats[:, 128:256]
                 misc = feats[:, 256:384]
                 fm[rows, :] = misc
-                g2m[rows, :] = norm(dot(silu(dot(misc, wemb[0])), wembo[2])).astype(BF16)
-                m2g[rows, :] = norm(dot(silu(dot(misc, wemb[1])), wembo[3])).astype(BF16)
+                g2m[rows, :] = norm(dot(silu_of_half(dot(misc, wemb[0])), wembo[2])).astype(BF16)
+                m2g[rows, :] = norm(dot(silu_of_half(dot(misc, wemb[1])), wembo[3])).astype(BF16)
             return carry
 
         lax.fori_loop(0, 4, embed_rows, 0)
         for sub in range(4):
             rows = pl.ds(sub * 256, 256)
-            mlat[rows, :] = norm(dot(silu(dot(mf[rows, :], wemb[2])), wembo[1])).astype(BF16)
+            mlat[rows, :] = norm(dot(silu_of_half(dot(mf[rows, :], wemb[2])), wembo[1])).astype(BF16)
         xs[2] = jnp.zeros(xs.shape[1:], BF16)
         for copy in weight_copies:
             copy.wait()
+
+        def halve(layer, carry):
+            wei[layer] = wei[layer] * 0.5
+            wni[layer] = wni[layer] * 0.5
+            return carry
+
+        lax.fori_loop(0, layers, halve, 0)
+        wsh[0] = wgs[0] * 0.5
+        wsh[1] = woh[...] * 0.5
 
         def en_copy(hop, half):
             dest = lax.rem(me + hop, group)
@@ -156,14 +168,19 @@
             for sub in range(0, blocks * 64, SUB):
                 rows = slice(sub, sub + SUB)
                 old = elat[k, rows, :]
-                pre = dot(old, w_first) + (send[rows] + recv[rows, :])
-                elat[k, rows, :] = residual(old, norm(dot(silu(pre), w_second)))
+                if RECV_MXU:
+                    node = hcur[sub // 64:(sub + SUB) // 64].reshape(SUB, 256)
+                    pre = dot(jnp.concatenate([old, node], axis=1), jnp.concatenate([w_first, wei[layer, 512:768, :]], axis=0)) + send[rows]
+                else:
+                    pre = dot(old, w_first) + (send[rows] + recv[rows, :])
+                elat[k, rows, :] = residual(old, norm(dot(silu_of_half(pre), w_second)))
 
         def mesh_layer(layer, carry):
             slot = lax.rem(layer, 2)
             h = hcur[...].reshape(blocks * 64, 256)
             proj[:, 8:72, :] = dot(h, wei[layer, 256:512, :]).reshape(blocks, 64, 256)
-            recv[...] = dot(h, wei[layer, 512:768, :])
+            if not RECV_MXU:
+                recv[...] = dot(h, wei[layer, 512:768, :])
             for k, shift in ((2, 1), (3, -1), (4, 4), (5, -4)):
                 edge_update(layer, k, rolled(shift))
             for copy in halo_copies(slot):
@@ -184,11 +201,15 @@
             for sub in range(0, blocks, SUB // 64):
                 node = hcur[sub:sub + SUB // 64].reshape(SUB, 256)
                 rows = slice(sub * 64, sub * 64 + SUB)
-                total = elat[0, rows, :].astype(F32)
-                for k in range(1, 6):
-                    total = total + elat[k, rows, :].astype(F32)
+                if SUM_MXU:
+                    edges = jnp.concatenate([elat[k, rows, :] for k in range(6)], axis=1)
+                    total = dot(edges, jnp.concatenate([perms[2]] * 6, axis=0))
+                else:
+                    total = elat[0, rows, :].astype(F32)
+                    for k in range(1, 6):
+                        total = total + elat[k, rows, :].astype(F32)
                 pre = dot(node, wni[layer, 0:256, :]) + dot(total.astype(BF16), wni[layer, 256:512, :])
-                new = residual(node, norm(dot(silu(pre), wno[layer])))
+                new = residual(node, norm(dot(silu_of_half(pre), wno[layer])))
                 hcur[sub:sub + SUB // 64] = new.reshape(SUB // 64, 64, 256)
 
             @pl.when(layer < layers - 2)
@@ -198,42 +219,43 @@
 
         def forecast(step, carry):
             def encode(it, carry):
-                for q in range(2):
-                    hop = 2 * it + 1 + q
-                    dest = lax.rem(me + hop, group)
-                    esums = []
-                    nodes = []
+                esums = []
+                nodes = []
+                dests = [lax.rem(me + PER * it + 1 + q, group) for q in range(PER)]
+                for dest in dests:
                     for half in range(2):
                         chunk = half * group + dest
                         rows = pl.ds(pl.multiple_of(chunk * 256, 256), 256)
                         mrows = pl.ds(pl.multiple_of(chunk * 64, 64), 64)
                         feats = jnp.concatenate([xs[step, rows, :], xs[step + 1, rows, :]], axis=1)
                         pre = dot(feats, wg[step, 0:256, :]) + dot(fm[rows, :], wg[step, 256:384, :])
-                        lat = norm(dot(silu(pre), wembo[0])).astype(BF16)
+                        lat = norm(dot(silu_of_half(pre), wembo[0])).astype(BF16)
                         glat[rows, :] = lat
                         node = mlat[mrows, :]
                         term = dot(node, wei[0, 512:768, :])
                         old = g2m[rows, :]
                         pre = dot(old, wei[0, 0:256, :]) + dot(lat, wei[0, 256:512, :])
                         pre = pre + jnp.concatenate([term] * 4, axis=0)
-                        edge = residual(old, norm(dot(silu(pre), weo[0]))).astype(F32)
+                        edge = residual(old, norm(dot(silu_of_half(pre), weo[0]))).astype(F32)
                         esums.append((edge[0:64] + edge[64:128] + edge[128:192] + edge[192:256]).astype(BF16))
                         nodes.append(node)
-                    node = jnp.concatenate(nodes, axis=0)
-                    pre = dot(node, wni[0, 0:256, :]) + dot(jnp.concatenate(esums, axis=0), wni[0, 256:512, :])
-                    new = residual(node, norm(dot(silu(pre), wno[0])))
-                    for half in range(2):
-                        hsend[half, dest] = new[half * 64:half * 64 + 64]
-                for half in range(2):
-                    en_copy(2 * it + 1, half).start()
-
-                @pl.when(it < group // 2 - 1)
+                for lo in range(0, 2 * PER, 4):
+                    node = jnp.concatenate(nodes[lo:lo + 4], axis=0)
+                    pre = dot(node, wni[0, 0:256, :]) + dot(jnp.concatenate(esums[lo:lo + 4], axis=0), wni[0, 256:512, :])
+                    new = residual(node, norm(dot(silu_of_half(pre), wno[0])))
+                    for q in range(4):
+                        hsend[q % 2, dests[(lo + q) // 2]] = new[q * 64:q * 64 + 64]
+                for q in range(PER - 1):
+                    for half in range(2):
+                        en_copy(PER * it + 1 + q, half).start()
+
+                @pl.when(it < group // PER - 1)
                 def _():
                     for half in range(2):
-                        en_copy(2 * it + 2, half).start()
+                        en_copy(PER * it + PER, half).start()
                 return carry
 
-            lax.fori_loop(0, group // 2, encode, 0)
+            lax.fori_loop(0, group // PER, encode, 0)
 
             @pl.when(step == 0)
             def _():
@@ -245,7 +267,7 @@
                 def embed_edges(k, carry):
                     for sub in range(0, blocks, 4):
                         feats = efl[sub:sub + 4].reshape(256, 128)
-                        ebase[k, sub * 64:sub * 64 + 256, :] = norm(dot(silu(dot(feats, wemb[3 + k])), wembo[4])).astype(BF16)
+                        ebase[k, sub * 64:sub * 64 + 256, :] = norm(dot(silu_of_half(dot(feats, wemb[3 + k])), wembo[4])).astype(BF16)
                     return carry
 
                 lax.fori_loop(0, 6, embed_edges, 0)
@@ -275,7 +297,7 @@
                 for sub in range(4):
                     rows = pl.ds(pl.multiple_of((it * 4 + sub) * 256, 256), 256)
                     old = glat[rows, :]
-                    gcur[rows, :] = residual(old, norm(dot(silu(dot(old, wgs[0])), wgs[1])))
+                    gcur[rows, :] = residual(old, norm(dot(silu_of_half(dot(old, wsh[0])), wgs[1])))
                 return carry
 
             lax.fori_loop(0, 4, self_update, 0)
@@ -286,17 +308,18 @@
 
             def decode(it, carry):
                 last = layers - 1
-                for half in range(2):
-                    de_arrival(lax.rem(me + 2 * it + 1, group), half).wait_recv()
-
-                @pl.when(it < group // 2 - 1)
+                for q in range(PER - 1):
+                    for half in range(2):
+                        de_arrival(lax.rem(me + PER * it + 1 + q, group), half).wait_recv()
+
+                @pl.when(it < group // PER - 1)
                 def _():
                     for half in range(2):
-                        de_arrival(lax.rem(me + 2 * it + 2, group), half).wait_recv()
+                        de_arrival(lax.rem(me + PER * it + PER, group), half).wait_recv()
 
                 work = []
-                for q in range(2):
-                    source = lax.rem(me + 2 * it + 1 + q, group)
+                for q in range(PER):
+                    source = lax.rem(me + PER * it + 1 + q, group)
                     for half in range(2):
                         rows = pl.ds(pl.multiple_of((half * group + source) * 256, 256), 256)
                         work.append((rows, hd[half, source], m2g[rows, :], gcur[rows, :], xst[step, rows, :]))
@@ -305,10 +328,10 @@
                     term = dot(node, wei[last, 256:512, :])
                     pre = dot(old, wei[last, 0:256, :]) + dot(grid, wei[last, 512:768, :])
                     pre = pre + jnp.concatenate([term] * 4, axis=0)
-                    edge = residual(old, norm(dot(silu(pre), weo[last])))
+                    edge = residual(old, norm(dot(silu_of_half(pre), weo[last])))
                     pre = dot(grid, wni[last, 0:256, :]) + dot(edge, wni[last, 256:512, :])
-                    out = residual(grid, norm(dot(silu(pre), wno[last])))
-                    hidden = silu(dot(out, woh[...]))
+                    out = residual(grid, norm(dot(silu_of_half(pre), wno[last])))
+                    hidden = silu_of_half(dot(out, wsh[1]))
                     hidden = dot(perms[1], hidden).astype(BF16)
                     new = state + stats[3:4, :] * dot(hidden, wof[...]) + stats[2:3, :]
                     scaled = ((new - stats[0:1, :]) / stats[1:2, :]).astype(BF16)
@@ -318,7 +341,7 @@
                     xs[2, rows, 0:scaled.shape[1]] = scaled
                 return carry
 
-            lax.fori_loop(0, group // 2, decode, 0)
+            lax.fori_loop(0, group // PER, decode, 0)
             for hop in range(1, group):
                 for half in range(2):
                     de_copy(hop, half).wait_send()
@@ -374,9 +397,9 @@
         w_force = w_grid_in[2 * variables:2 * variables + force]
         w_static = w_grid_in[2 * variables + force:]
         w_state = placed(w_grid_in[:variables], 0, 384) + placed(w_grid_in[variables:2 * variables], 128, 384) + placed(w_static, 256 + 2 * force, 384)
-        w_grid = jnp.stack([w_state + placed(w_force, 256 + force * s, 384) for s in range(2)])
+        w_grid = 0.5 * jnp.stack([w_state + placed(w_force, 256 + force * s, 384) for s in range(2)])
         at_g2m = 2 * force + static
-        w_embed = jnp.stack([placed(w_eemb_in[0], at_g2m, 128), placed(w_eemb_in[1], at_g2m + edge_lanes, 128), placed(w_mesh_in, 0, 128)]
+        w_embed = 0.5 * jnp.stack([placed(w_eemb_in[0], at_g2m, 128), placed(w_eemb_in[1], at_g2m + edge_lanes, 128), placed(w_mesh_in, 0, 128)]
                             + [placed(w_eemb_in[2], edge_lanes * k, 128) for k in range(6)])
         perms = jnp.asarray(row_permutation(), BF16)
 
@@ -400,11 +423,11 @@
                 pltpu.VMEM((2, group, 64, latent), BF16), pltpu.VMEM((blocks, 64, latent), BF16),
                 pltpu.VMEM((blocks, 64, latent), BF16), pltpu.VMEM((2, group, 64, latent), BF16),
                 pltpu.VMEM((blocks, 80, latent), F32), pltpu.VMEM((mesh_dev, latent), F32),
-                pltpu.VMEM((2, 2, blocks, latent), BF16), pltpu.VMEM((2, 2, blocks, latent), BF16), pltpu.VMEM((2, blocks, latent), F32),
+                pltpu.VMEM((2, 2, blocks, latent), BF16), pltpu.VMEM((2, 2, blocks, latent), BF16), pltpu.VMEM((2, blocks, latent), F32), pltpu.VMEM((2, latent, latent), BF16),
                 dma((4,)), dma, dma((2,)), dma((group, 2)), dma((group, 2)), dma((group, 2)), dma((group, 2)),
                 dma((group, 2)), dma((group, 2)), dma((2, 2)), dma((2, 2)),
             ],
-            compiler_params=pltpu.CompilerParams(collective_id=0, has_side_effects=True, vmem_limit_bytes=67043328),
+            compiler_params=pltpu.CompilerParams(collective_id=0, has_side_effects=True, flags=FLAGS, vmem_limit_bytes=67043328),
         )(feats, x_cur, edge_rows, mesh_rows, norm_stats, perms, w_grid, w_embed, w_embed_out, w_edge_in, w_edge_out, w_node_in, w_node_out,
           w_grid_self, w_out_hidden, w_out_final)
 

time: 341 us -> 322 us (0.944)
  Pallas kernels: 302 us -> 288 us
  local copies, waits for them, and re-layouts: 28 us -> 22.3 us
    pallas_call x1, Pallas kernels: 302 us -> 288 us  [local_run(): pl.pallas_call(kernel, out_shape=(state, state), in_specs=[vmem, anywhere...]
    unnamed x26, local copies, waits for them, and re-layouts: 12.7 us -> 7.69 us
  transfers between devices with their start and end apart: 2 -> 2, of which waited for: 0 -> 0; matrix products, arithmetic and copies ran while one was open for 8% -> 6% of each run, Pallas kernels for 0% -> 0%
where the time goes in v2:
time: 322 us
  Pallas kernels  288 us (89%)
  local copies, waits for them, and re-layouts  22.3 us (7%)
  other arithmetic  6.88 us (2%)
  starting transfers between devices  4.15 us (1%)
    pallas_call x1, Pallas kernels, local_run(): pl.pallas_call(kernel, out_shape=(state, state), in_specs=[vmem, anywhere...  288 us
    unnamed x26, local copies, waits for them, and re-layouts  7.69 us
  transfers between devices with their start and end apart: 2, of which 0 were waited for; matrix products, arithmetic and copies ran while one was open for 6% of the time, Pallas kernels for 0%

profile of v2, /device:TPU:113, one launch (start us, length us, event | category | flops | bytes accessed | tf_op | source)
XLA Modules:
  0.0 321.7 jit_solution(11372774470631032527)
XLA Ops:
  0.6 0.7 fusion.9
  1.3 0.7 collective-permute-start.1
  2.1 0.8 fusion.8
  2.9 3.4 %collective-permute-start = (bf16[2048,4]{0,1:T(4,128)(2,1)S(1)}, bf16[2048,4]{0,1:T(4,128)(2,1)S(1)}, u32[]{:S(2)}, u32[]{:S(2)}) collective-permute-start(bf16[2048,4]{0,1:T(4,128)(2,1)S(1)} %get-tuple-element.17), channel_id=1, source_target_pairs={{0,7},{1,0},{2,1},{3,2},{4,3},{5,4},{6,5},{7,6},{8,15},{9,8},{10,9... | collective-permute-start | bytes 49160 | tf_op jit(solution)/shard_map/ppermute | solution.py:372
  6.3 0.8 fusion.7
  7.1 0.9 fusion.6
  7.9 0.8 slice_bitcast_fusion.5
  8.7 0.7 slice_bitcast_fusion.2
  9.4 1.0 copy.72
  10.4 0.7 bitcast_dynamic-update-slice_fusion.6
  11.2 0.9 broadcast_multiply_fusion.wemb
  12.1 1.8 copy.61.xc_hbm
  13.9 0.0 copy-start
  13.9 3.4 %copy.59 = f32[4096,78]{1,0:T(8,128)} copy(f32[4096,78]{0,1:T(8,128)} %param.21) | data formatting | bytes 2555904 | tf_op args[0]
  17.4 0.0 copy-start.4
  17.4 0.0 copy-start.5
  17.4 0.0 copy-start.3
  17.4 0.0 copy-start.6
  17.4 3.1 divide_convert_fusion.1
  20.5 0.0 copy-done
  20.5 0.8 maximum_multiply_fusion.wg
  21.3 0.0 copy-done.4
  21.4 0.0 copy-done.5
  21.4 0.0 copy-done.3
  21.4 0.0 copy-done.6
  21.4 0.7 copy.68.wof
  22.2 0.0 copy-start.1
  22.2 0.9 convert_element_type.61
  23.1 0.9 copy.65
  24.0 0.8 pad.81.ef_hbm
  24.8 0.0 collective-permute-done.1
  24.8 0.1 convert_element_type.64
  24.9 0.9 copy.66
  25.8 0.8 pad.82
  26.6 0.0 collective-permute-done
  26.6 0.5 concatenate.17
  27.1 0.5 copy.64
  27.6 0.0 copy-done.1
  27.6 2.0 fusion.5.f0
  29.6 287.5 %shard_map.212 = (f32[4096,78]{1,0:T(8,128)}, f32[4096,78]{1,0:T(8,128)}) custom-call(bf16[4096,384]{1,0:T(8,128)(2,1)} %fusion.5.f0, f32[4096,78]{1,0:T(8,128)} %copy-done, bf16[2,8,64,128]{3,2,1,0:T(8,128)(2,1)} %pad.81.ef_hbm, bf16[1024,128]{1,0:T(8,128)(2,1)} %bitcast.46, f32[4,78]{1,0:T(4,128)} %stats.1, bf16[3,256,256]{2,1,0:T(8,128)(2,1)} %constant.10.clone.perms, ...), custom_call_target="tpu_custom_call" | custom-call | tf_op jit(solution)/shard_map/pallas_call | solution.py:410
  317.1 0.0 copy-start.2
  317.1 2.9 copy.69
  320.0 0.0 copy-done.2
  320.0 1.7 copy.70
  (15 shorter events, 0.2 us)
Async XLA Ops:
  1.3 23.4 %collective-permute-start.1 = (bf16[512,3]{0,1:T(4,128)(2,1)S(1)}, bf16[512,3]{0,1:T(4,128)(2,1)S(1)}, u32[]{:S(2)}, u32[]{:S(2)}) collective-permute-start(bf16[512,3]{0,1:T(4,128)(2,1)S(1)} %get-tuple-element.21), channel_id=1, source_target_pairs={{0,7},{1,0},{2,1},{3,2},{4,3},{5,4},{6,5},{7,6},{8,15},{9,8},{10,9... | collective-permute-start | bytes 9224 | tf_op jit(solution)/shard_map/ppermute | solution.py:372
  2.9 23.7 %collective-permute-start = (bf16[2048,4]{0,1:T(4,128)(2,1)S(1)}, bf16[2048,4]{0,1:T(4,128)(2,1)S(1)}, u32[]{:S(2)}, u32[]{:S(2)}) collective-permute-start(bf16[2048,4]{0,1:T(4,128)(2,1)S(1)} %get-tuple-element.17), channel_id=1, source_target_pairs={{0,7},{1,0},{2,1},{3,2},{4,3},{5,4},{6,5},{7,6},{8,15},{9,8},{10,9... | collective-permute-start | bytes 49160 | tf_op jit(solution)/shard_map/ppermute | solution.py:372
  13.9 6.6 %copy-start = (f32[4096,78]{1,0:T(8,128)}, f32[4096,78]{1,0:T(8,128)S(1)}, u32[]{:S(2)}) copy-start(f32[4096,78]{1,0:T(8,128)S(1)} %copy.61.xc_hbm) | copy-start | bytes 3833860
  17.4 4.0 %copy-start.4 = (f32[4096,3]{0,1:T(4,128)S(1)}, f32[4096,3]{0,1:T(4,128)}, u32[]{:S(2)}) copy-start(f32[4096,3]{0,1:T(4,128)} %param.24) | copy-start | bytes 147460
  17.4 4.0 %copy-start.5 = (f32[4096,4]{0,1:T(4,128)S(1)}, f32[4096,4]{0,1:T(4,128)}, u32[]{:S(2)}) copy-start(f32[4096,4]{0,1:T(4,128)} %param.26) | copy-start | bytes 196612
  17.4 4.0 %copy-start.3 = (f32[1024,6,4]{0,2,1:T(4,128)S(1)}, f32[1024,6,4]{0,2,1:T(4,128)}, u32[]{:S(2)}) copy-start(f32[1024,6,4]{0,2,1:T(4,128)} %param.28) | copy-start | bytes 294916
  17.4 4.0 %copy-start.6 = (bf16[256,78]{0,1:T(8,128)(2,1)S(1)}, bf16[256,78]{0,1:T(8,128)(2,1)}, u32[]{:S(2)}) copy-start(bf16[256,78]{0,1:T(8,128)(2,1)} %param.40) | copy-start | bytes 119812
  22.2 5.4 %copy-start.1 = (bf16[4096,78]{1,0:T(8,128)(2,1)S(1)}, bf16[4096,78]{1,0:T(8,128)(2,1)}, u32[]{:S(2)}) copy-start(bf16[4096,78]{1,0:T(8,128)(2,1)} %get-tuple-element.28) | copy-start | bytes 1916932
  317.1 2.9 copy-start.2

commit v3 on v2

--- a/solution.py
+++ b/solution.py
@@ -10,9 +10,10 @@
 F32 = jnp.float32
 BF16 = jnp.bfloat16
 SUB = 256
+TAIL = 256
 PER = 4
-RECV_MXU = False
-SUM_MXU = False
+WIDTH = 3
+TAIL_WIDTH = 4
 FLAGS = {}
 
 
@@ -27,6 +28,23 @@
 def norm(y):
     z = y - jnp.mean(y, axis=-1, keepdims=True)
     return z * lax.rsqrt(jnp.mean(z * z, axis=-1, keepdims=True) + 1e-5)
+
+
+def staggered(tasks, width):
+    waiting = list(tasks)
+    active = []
+    while waiting or active:
+        if waiting and len(active) < width:
+            active.append(waiting.pop(0))
+        for task in list(active):
+            if next(task, "done") == "done":
+                active.remove(task)
+
+
+def together(tasks):
+    active = list(tasks)
+    while active:
+        active = [task for task in active if next(task, "done") != "done"]
 
 
 def residual(base, update):
@@ -39,7 +57,7 @@
         for j in range(8):
             for i in range(8):
                 perm[r * 64 + j * 8 + i, (i * 8 + j) * 4 + r] = 1.0
-    return np.stack([perm, perm.T, np.eye(256, dtype=np.float32)])
+    return np.stack([perm, perm.T])
 
 
 def solution(mesh):
@@ -85,23 +103,42 @@
                 ef_copy(hop, half).start()
             ef_keep(half).start()
 
+        def embed_task(rows):
+            feats = dot(perms[0], f0[rows, :])
+            yield
+            feats = feats.astype(BF16)
+            xs[0, rows, :] = feats[:, 0:128]
+            xs[1, rows, :] = feats[:, 128:256]
+            misc = feats[:, 256:384]
+            fm[rows, :] = misc
+            first = dot(misc, wemb[0])
+            second = dot(misc, wemb[1])
+            yield
+            first = dot(silu_of_half(first), wembo[2])
+            second = dot(silu_of_half(second), wembo[3])
+            yield
+            g2m[rows, :] = norm(first).astype(BF16)
+            m2g[rows, :] = norm(second).astype(BF16)
+
         def embed_rows(it, carry):
-            for sub in range(4):
-                base = pl.multiple_of((it * 4 + sub) * 256, 256)
-                rows = pl.ds(base, 256)
-                feats = dot(perms[0], f0[rows, :]).astype(BF16)
-                xs[0, rows, :] = feats[:, 0:128]
-                xs[1, rows, :] = feats[:, 128:256]
-                misc = feats[:, 256:384]
-                fm[rows, :] = misc
-                g2m[rows, :] = norm(dot(silu_of_half(dot(misc, wemb[0])), wembo[2])).astype(BF16)
-                m2g[rows, :] = norm(dot(silu_of_half(dot(misc, wemb[1])), wembo[3])).astype(BF16)
+            together(embed_task(pl.ds(pl.multiple_of((it * 4 + sub) * 256, 256), 256)) for sub in range(4))
             return carry
 
         lax.fori_loop(0, 4, embed_rows, 0)
-        for sub in range(4):
-            rows = pl.ds(sub * 256, 256)
-            mlat[rows, :] = norm(dot(silu_of_half(dot(mf[rows, :], wemb[2])), wembo[1])).astype(BF16)
+
+        def plain_task(get, put, w_first, w_second):
+            y = dot(get(), w_first)
+            yield
+            y = dot(silu_of_half(y), w_second)
+            yield
+            put(norm(y))
+
+        def mesh_task(rows):
+            def put(y):
+                mlat[rows, :] = y.astype(BF16)
+            return plain_task(lambda: mf[rows, :], put, wemb[2], wembo[1])
+
+        together(mesh_task(pl.ds(sub * 256, 256)) for sub in range(4))
         xs[2] = jnp.zeros(xs.shape[1:], BF16)
         for copy in weight_copies:
             copy.wait()
@@ -157,32 +194,60 @@
             for copy in halo_copies(slot):
                 copy.start()
 
-        def rolled(shift):
-            cut = shift % blocks
-            return jnp.concatenate([proj[cut:, 8:72, :], proj[:cut, 8:72, :]], axis=0)
-
-        def edge_update(layer, k, send):
-            send = send.reshape(blocks * 64, 256)
-            w_first = wei[layer, 0:256, :]
-            w_second = weo[layer]
-            for sub in range(0, blocks * 64, SUB):
-                rows = slice(sub, sub + SUB)
-                old = elat[k, rows, :]
-                if RECV_MXU:
-                    node = hcur[sub // 64:(sub + SUB) // 64].reshape(SUB, 256)
-                    pre = dot(jnp.concatenate([old, node], axis=1), jnp.concatenate([w_first, wei[layer, 512:768, :]], axis=0)) + send[rows]
-                else:
-                    pre = dot(old, w_first) + (send[rows] + recv[rows, :])
-                elat[k, rows, :] = residual(old, norm(dot(silu_of_half(pre), w_second)))
+        def edge_task(layer, k, sub, size, send):
+            rows = slice(sub, sub + size)
+            old = elat[k, rows, :]
+            pre = dot(old, wei[layer, 0:256, :]) + (send + recv[rows, :])
+            yield
+            y = dot(silu_of_half(pre), weo[layer])
+            yield
+            elat[k, rows, :] = residual(old, norm(y))
+
+        def project(layer, lo, hi):
+            h = hcur[lo:hi].reshape((hi - lo) * 64, 256)
+            return dot(h, wei[layer, 256:512, :]), dot(h, wei[layer, 512:768, :])
+
+        def put_projections(lo, hi, send, receive):
+            proj[lo:hi, 8:72, :] = send.reshape(hi - lo, 64, 256)
+            recv[lo * 64:hi * 64, :] = receive
+
+        def tail_task(layer, lo, hi):
+            size = (hi - lo) * 64
+            rows = slice(lo * 64, hi * 64)
+            olds = [elat[k, rows, :] for k in range(2)]
+            sends = [proj[lo:hi, 16:80, :].reshape(size, 256), proj[lo:hi, 0:64, :].reshape(size, 256)]
+            pres = [dot(old, wei[layer, 0:256, :]) + (send + recv[rows, :]) for old, send in zip(olds, sends)]
+            total = elat[2, rows, :].astype(F32)
+            for k in range(3, 6):
+                total = total + elat[k, rows, :].astype(F32)
+            yield
+            ys = [dot(silu_of_half(pre), weo[layer]) for pre in pres]
+            yield
+            for k in range(2):
+                new = residual(olds[k], norm(ys[k]))
+                elat[k, rows, :] = new
+                total = total + new.astype(F32)
+            node = hcur[lo:hi].reshape(size, 256)
+            pre = dot(node, wni[layer, 0:256, :]) + dot(total.astype(BF16), wni[layer, 256:512, :])
+            yield
+            y = dot(silu_of_half(pre), wno[layer])
+            yield
+            new = residual(node, norm(y))
+            hcur[lo:hi] = new.reshape(hi - lo, 64, 256)
+            send = dot(new, wei[layer + 1, 256:512, :])
+            receive = dot(new, wei[layer + 1, 512:768, :])
+            yield
+            put_projections(lo, hi, send, receive)
+
+        def rolled(shift, sub, size):
+            lo, count = sub // 64, size // 64
+            picks = [(lo + q + shift) % blocks for q in range(count)]
+            return jnp.concatenate([proj[b, 8:72, :] for b in picks], axis=0)
 
         def mesh_layer(layer, carry):
             slot = lax.rem(layer, 2)
-            h = hcur[...].reshape(blocks * 64, 256)
-            proj[:, 8:72, :] = dot(h, wei[layer, 256:512, :]).reshape(blocks, 64, 256)
-            if not RECV_MXU:
-                recv[...] = dot(h, wei[layer, 512:768, :])
-            for k, shift in ((2, 1), (3, -1), (4, 4), (5, -4)):
-                edge_update(layer, k, rolled(shift))
+            staggered((edge_task(layer, k, sub, SUB, rolled(shift, sub, SUB))
+                       for k, shift in ((2, 1), (3, -1), (4, 4), (5, -4)) for sub in range(0, blocks * 64, SUB)), WIDTH)
             for copy in halo_copies(slot):
                 copy.wait_recv()
             for copy in halo_copies(slot):
@@ -196,21 +261,7 @@
             for b in range(blocks):
                 proj[b, 0:8, :] = jnp.where(sublane == 0, stage[0, b:b + 1, :], pltpu.roll(proj[b, 64:72, :], 1, 0))
                 proj[b, 72:80, :] = jnp.where(sublane == 7, stage[1, b:b + 1, :], pltpu.roll(proj[b, 8:16, :], 7, 0))
-            edge_update(layer, 0, proj[:, 16:80, :])
-            edge_update(layer, 1, proj[:, 0:64, :])
-            for sub in range(0, blocks, SUB // 64):
-                node = hcur[sub:sub + SUB // 64].reshape(SUB, 256)
-                rows = slice(sub * 64, sub * 64 + SUB)
-                if SUM_MXU:
-                    edges = jnp.concatenate([elat[k, rows, :] for k in range(6)], axis=1)
-                    total = dot(edges, jnp.concatenate([perms[2]] * 6, axis=0))
-                else:
-                    total = elat[0, rows, :].astype(F32)
-                    for k in range(1, 6):
-                        total = total + elat[k, rows, :].astype(F32)
-                pre = dot(node, wni[layer, 0:256, :]) + dot(total.astype(BF16), wni[layer, 256:512, :])
-                new = residual(node, norm(dot(silu_of_half(pre), wno[layer])))
-                hcur[sub:sub + SUB // 64] = new.reshape(SUB // 64, 64, 256)
+            staggered((tail_task(layer, lo, lo + TAIL // 64) for lo in range(0, blocks, TAIL // 64)), TAIL_WIDTH)
 
             @pl.when(layer < layers - 2)
             def _():
@@ -218,33 +269,51 @@
             return carry
 
         def forecast(step, carry):
+            def encode_task(dest, half):
+                chunk = half * group + dest
+                rows = pl.ds(pl.multiple_of(chunk * 256, 256), 256)
+                feats = jnp.concatenate([xs[step, rows, :], xs[step + 1, rows, :]], axis=1)
+                node = mlat[pl.ds(pl.multiple_of(chunk * 64, 64), 64), :]
+                old = g2m[rows, :]
+                pre = dot(feats, wg[step, 0:256, :]) + dot(fm[rows, :], wg[step, 256:384, :])
+                yield
+                y = dot(silu_of_half(pre), wembo[0])
+                yield
+                lat = norm(y).astype(BF16)
+                glat[rows, :] = lat
+                pre = dot(old, wei[0, 0:256, :]) + dot(lat, wei[0, 256:512, :])
+                term = dot(node, wei[0, 512:768, :])
+                yield
+                pre = pre + jnp.concatenate([term] * 4, axis=0)
+                y = dot(silu_of_half(pre), weo[0])
+                yield
+                edge = residual(old, norm(y)).astype(F32)
+                return node, (edge[0:64] + edge[64:128] + edge[128:192] + edge[192:256]).astype(BF16)
+
+            def encode_group(pairs):
+                results = []
+
+                def run(dest, half):
+                    results.append((yield from encode_task(dest, half)))
+
+                active = [run(dest, half) for dest, half in pairs]
+                while active:
+                    active = [task for task in active if next(task, "done") != "done"]
+                    yield
+                node = jnp.concatenate([r[0] for r in results], axis=0)
+                esum = jnp.concatenate([r[1] for r in results], axis=0)
+                pre = dot(node, wni[0, 0:256, :]) + dot(esum, wni[0, 256:512, :])
+                yield
+                y = dot(silu_of_half(pre), wno[0])
+                yield
+                new = residual(node, norm(y))
+                for q, (dest, half) in enumerate(pairs):
+                    hsend[half, dest] = new[q * 64:q * 64 + 64]
+
             def encode(it, carry):
-                esums = []
-                nodes = []
                 dests = [lax.rem(me + PER * it + 1 + q, group) for q in range(PER)]
-                for dest in dests:
-                    for half in range(2):
-                        chunk = half * group + dest
-                        rows = pl.ds(pl.multiple_of(chunk * 256, 256), 256)
-                        mrows = pl.ds(pl.multiple_of(chunk * 64, 64), 64)
-                        feats = jnp.concatenate([xs[step, rows, :], xs[step + 1, rows, :]], axis=1)
-                        pre = dot(feats, wg[step, 0:256, :]) + dot(fm[rows, :], wg[step, 256:384, :])
-                        lat = norm(dot(silu_of_half(pre), wembo[0])).astype(BF16)
-                        glat[rows, :] = lat
-                        node = mlat[mrows, :]
-                        term = dot(node, wei[0, 512:768, :])
-                        old = g2m[rows, :]
-                        pre = dot(old, wei[0, 0:256, :]) + dot(lat, wei[0, 256:512, :])
-                        pre = pre + jnp.concatenate([term] * 4, axis=0)
-                        edge = residual(old, norm(dot(silu_of_half(pre), weo[0]))).astype(F32)
-                        esums.append((edge[0:64] + edge[64:128] + edge[128:192] + edge[192:256]).astype(BF16))
-                        nodes.append(node)
-                for lo in range(0, 2 * PER, 4):
-                    node = jnp.concatenate(nodes[lo:lo + 4], axis=0)
-                    pre = dot(node, wni[0, 0:256, :]) + dot(jnp.concatenate(esums[lo:lo + 4], axis=0), wni[0, 256:512, :])
-                    new = residual(node, norm(dot(silu_of_half(pre), wno[0])))
-                    for q in range(4):
-                        hsend[q % 2, dests[(lo + q) // 2]] = new[q * 64:q * 64 + 64]
+                pairs = [(dest, half) for dest in dests for half in range(2)]
+                staggered((encode_group(pairs[lo:lo + 4]) for lo in range(0, 2 * PER, 4)), 4)
                 for q in range(PER - 1):
                     for half in range(2):
                         en_copy(PER * it + 1 + q, half).start()
@@ -265,9 +334,12 @@
                     ef_keep(half).wait()
 
                 def embed_edges(k, carry):
-                    for sub in range(0, blocks, 4):
-                        feats = efl[sub:sub + 4].reshape(256, 128)
-                        ebase[k, sub * 64:sub * 64 + 256, :] = norm(dot(silu_of_half(dot(feats, wemb[3 + k])), wembo[4])).astype(BF16)
+                    def edge_embed_task(sub):
+                        def put(y):
+                            ebase[k, sub * 64:sub * 64 + 256, :] = y.astype(BF16)
+                        return plain_task(lambda: efl[sub:sub + 4].reshape(256, 128), put, wemb[3 + k], wembo[4])
+
+                    together(edge_embed_task(sub) for sub in range(0, blocks, 4))
                     return carry
 
                 lax.fori_loop(0, 6, embed_edges, 0)
@@ -286,6 +358,7 @@
             for half in range(2):
                 hcur[block_of(me, 1 + half)] = hsend[half, me]
             send_halo(1)
+            put_projections(0, blocks, *project(1, 0, blocks))
             lax.fori_loop(1, layers - 1, mesh_layer, 0)
             for hop in range(1, group):
                 for half in range(2):
@@ -293,11 +366,15 @@
             for half in range(2):
                 hd[half, me] = hcur[block_of(me, 1 + half)]
 
+            def self_task(rows):
+                old = glat[rows, :]
+
+                def put(y):
+                    gcur[rows, :] = residual(old, y)
+                return plain_task(lambda: old, put, wsh[0], wgs[1])
+
             def self_update(it, carry):
-                for sub in range(4):
-                    rows = pl.ds(pl.multiple_of((it * 4 + sub) * 256, 256), 256)
-                    old = glat[rows, :]
-                    gcur[rows, :] = residual(old, norm(dot(silu_of_half(dot(old, wsh[0])), wgs[1])))
+                together(self_task(pl.ds(pl.multiple_of((it * 4 + sub) * 256, 256), 256)) for sub in range(4))
                 return carry
 
             lax.fori_loop(0, 4, self_update, 0)
@@ -323,22 +400,32 @@
                     for half in range(2):
                         rows = pl.ds(pl.multiple_of((half * group + source) * 256, 256), 256)
                         work.append((rows, hd[half, source], m2g[rows, :], gcur[rows, :], xst[step, rows, :]))
-                done = []
-                for rows, node, old, grid, state in work:
+                def decode_task(rows, node, old, grid, state):
+                    pre = dot(old, wei[last, 0:256, :]) + dot(grid, wei[last, 512:768, :])
                     term = dot(node, wei[last, 256:512, :])
-                    pre = dot(old, wei[last, 0:256, :]) + dot(grid, wei[last, 512:768, :])
+                    yield
                     pre = pre + jnp.concatenate([term] * 4, axis=0)
-                    edge = residual(old, norm(dot(silu_of_half(pre), weo[last])))
+                    y = dot(silu_of_half(pre), weo[last])
+                    yield
+                    edge = residual(old, norm(y))
                     pre = dot(grid, wni[last, 0:256, :]) + dot(edge, wni[last, 256:512, :])
-                    out = residual(grid, norm(dot(silu_of_half(pre), wno[last])))
-                    hidden = silu_of_half(dot(out, wsh[1]))
-                    hidden = dot(perms[1], hidden).astype(BF16)
-                    new = state + stats[3:4, :] * dot(hidden, wof[...]) + stats[2:3, :]
-                    scaled = ((new - stats[0:1, :]) / stats[1:2, :]).astype(BF16)
-                    done.append((rows, new, dot(perms[0], scaled).astype(BF16)))
-                for rows, new, scaled in done:
+                    yield
+                    y = dot(silu_of_half(pre), wno[last])
+                    yield
+                    out = residual(grid, norm(y))
+                    pre = dot(out, wsh[1])
+                    yield
+                    hidden = dot(perms[1], silu_of_half(pre))
+                    yield
+                    p = dot(hidden.astype(BF16), wof[...])
+                    yield
+                    new = state + stats[3:4, :] * p + stats[2:3, :]
+                    scaled = dot(perms[0], ((new - stats[0:1, :]) / stats[1:2, :]).astype(BF16))
+                    yield
                     xst[step + 1, rows, :] = new
-                    xs[2, rows, 0:scaled.shape[1]] = scaled
+                    xs[2, rows, 0:new.shape[1]] = scaled.astype(BF16)
+
+                staggered((decode_task(*args) for args in work), 2 * PER)
                 return carry
 
             lax.fori_loop(0, group // PER, decode, 0)

time: 322 us -> 283 us (0.88)
  Pallas kernels: 288 us -> 248 us
    pallas_call x1, Pallas kernels: 288 us -> 248 us  [local_run(): pl.pallas_call(kernel, out_shape=(state, state), in_specs=[vmem, anywhere...]
  transfers between devices with their start and end apart: 2 -> 2, of which waited for: 0 -> 0; matrix products, arithmetic and copies ran while one was open for 6% -> 7% of each run, Pallas kernels for 0% -> 0%
where the time goes in v3:
time: 283 us; the launch traced here: 282 us
  Pallas kernels  248 us (88%)
  local copies, waits for them, and re-layouts  22.3 us (8%)
  other arithmetic  6.88 us (2%)
  starting transfers between devices  4.15 us (1%)
    pallas_call x1, Pallas kernels, local_run(): pl.pallas_call(kernel, out_shape=(state, state), in_specs=[vmem, anywhere...  248 us
    unnamed x26, local copies, waits for them, and re-layouts  7.69 us
  transfers between devices with their start and end apart: 2, of which 0 were waited for; matrix products, arithmetic and copies ran while one was open for 7% of the time, Pallas kernels for 0%

profile of v3, /device:TPU:113, one launch (start us, length us, event | category | flops | bytes accessed | tf_op | source)
XLA Modules:
  0.0 282.2 jit_solution(11254650727567461546)
XLA Ops:
  0.6 0.7 fusion.9
  1.3 0.7 collective-permute-start.1
  2.1 0.8 fusion.8
  2.9 3.4 %collective-permute-start = (bf16[2048,4]{0,1:T(4,128)(2,1)S(1)}, bf16[2048,4]{0,1:T(4,128)(2,1)S(1)}, u32[]{:S(2)}, u32[]{:S(2)}) collective-permute-start(bf16[2048,4]{0,1:T(4,128)(2,1)S(1)} %get-tuple-element.17), channel_id=1, source_target_pairs={{0,7},{1,0},{2,1},{3,2},{4,3},{5,4},{6,5},{7,6},{8,15},{9,8},{10,9... | collective-permute-start | bytes 49160 | tf_op jit(solution)/shard_map/ppermute | solution.py:459
  6.3 0.8 fusion.7
  7.1 0.9 fusion.6
  7.9 0.8 slice_bitcast_fusion.5
  8.7 0.7 slice_bitcast_fusion.2
  9.4 1.0 copy.72
  10.4 0.7 bitcast_dynamic-update-slice_fusion.6
  11.2 0.9 broadcast_multiply_fusion.wemb
  12.1 1.8 copy.61.xc_hbm
  13.9 0.0 copy-start
  13.9 3.4 %copy.59 = f32[4096,78]{1,0:T(8,128)} copy(f32[4096,78]{0,1:T(8,128)} %param.21) | data formatting | bytes 2555904 | tf_op args[0]
  17.4 0.0 copy-start.4
  17.4 0.0 copy-start.5
  17.4 0.0 copy-start.3
  17.4 0.0 copy-start.6
  17.4 3.1 %divide_convert_fusion.1 = (bf16[4096,78]{1,0:T(8,128)(2,1)S(1)}, bf16[4096,78]{1,0:T(8,128)(2,1)}) fusion(f32[4096,78]{1,0:T(8,128)} %copy.59, f32[78]{0:T(128)S(1)} %get-tuple-element.26, f32[78]{0:T(128)S(1)} %get-tuple-element.25, f32[4096,78]{1,0:T(8,128)S(1)} %copy.61.xc_hbm), kind=kLoop, calls=%fused_computation.11 | loop fusion | flops 1916928 | bytes 3834480 | tf_op jit(solution)/shard_map/convert.22
  20.5 0.0 copy-done
  20.5 0.8 maximum_multiply_fusion.wg
  21.3 0.0 copy-done.4
  21.4 0.0 copy-done.5
  21.4 0.0 copy-done.3
  21.4 0.0 copy-done.6
  21.4 0.7 copy.68.wof
  22.2 0.0 copy-start.1
  22.2 0.9 convert_element_type.61
  23.1 0.9 copy.65
  24.0 0.8 pad.81.ef_hbm
  24.8 0.0 collective-permute-done.1
  24.8 0.1 convert_element_type.64
  24.9 0.9 copy.66
  25.8 0.8 pad.82
  26.6 0.0 collective-permute-done
  26.6 0.5 concatenate.17
  27.1 0.5 copy.64
  27.6 0.0 copy-done.1
  27.6 2.0 fusion.5.f0
  29.6 248.0 %shard_map.212 = (f32[4096,78]{1,0:T(8,128)}, f32[4096,78]{1,0:T(8,128)}) custom-call(bf16[4096,384]{1,0:T(8,128)(2,1)} %fusion.5.f0, f32[4096,78]{1,0:T(8,128)} %copy-done, bf16[2,8,64,128]{3,2,1,0:T(8,128)(2,1)} %pad.81.ef_hbm, bf16[1024,128]{1,0:T(8,128)(2,1)} %bitcast.46, f32[4,78]{1,0:T(4,128)} %stats.1, bf16[2,256,256]{2,1,0:T(8,128)(2,1)} %constant.10.clone.perms, ...), custom_call_target="tpu_custom_call" | custom-call | tf_op jit(solution)/shard_map/pallas_call | solution.py:497
  277.6 0.0 copy-start.2
  277.6 2.9 %copy.69 = f32[4096,78]{0,1:T(8,128)} copy(f32[4096,78]{1,0:T(8,128)} %get-tuple-element.8) | data formatting | bytes 2555904 | tf_op jit(solution)/shard_map/pallas_call | solution.py:497
  280.5 0.0 copy-done.2
  280.5 1.7 copy.70
  (15 shorter events, 0.2 us)
Async XLA Ops:
  1.3 23.4 %collective-permute-start.1 = (bf16[512,3]{0,1:T(4,128)(2,1)S(1)}, bf16[512,3]{0,1:T(4,128)(2,1)S(1)}, u32[]{:S(2)}, u32[]{:S(2)}) collective-permute-start(bf16[512,3]{0,1:T(4,128)(2,1)S(1)} %get-tuple-element.21), channel_id=1, source_target_pairs={{0,7},{1,0},{2,1},{3,2},{4,3},{5,4},{6,5},{7,6},{8,15},{9,8},{10,9... | collective-permute-start | bytes 9224 | tf_op jit(solution)/shard_map/ppermute | solution.py:459
  2.9 23.7 %collective-permute-start = (bf16[2048,4]{0,1:T(4,128)(2,1)S(1)}, bf16[2048,4]{0,1:T(4,128)(2,1)S(1)}, u32[]{:S(2)}, u32[]{:S(2)}) collective-permute-start(bf16[2048,4]{0,1:T(4,128)(2,1)S(1)} %get-tuple-element.17), channel_id=1, source_target_pairs={{0,7},{1,0},{2,1},{3,2},{4,3},{5,4},{6,5},{7,6},{8,15},{9,8},{10,9... | collective-permute-start | bytes 49160 | tf_op jit(solution)/shard_map/ppermute | solution.py:459
  13.9 6.6 %copy-start = (f32[4096,78]{1,0:T(8,128)}, f32[4096,78]{1,0:T(8,128)S(1)}, u32[]{:S(2)}) copy-start(f32[4096,78]{1,0:T(8,128)S(1)} %copy.61.xc_hbm) | copy-start | bytes 3833860
  17.4 4.0 %copy-start.4 = (f32[4096,3]{0,1:T(4,128)S(1)}, f32[4096,3]{0,1:T(4,128)}, u32[]{:S(2)}) copy-start(f32[4096,3]{0,1:T(4,128)} %param.24) | copy-start | bytes 147460
  17.4 4.0 %copy-start.5 = (f32[4096,4]{0,1:T(4,128)S(1)}, f32[4096,4]{0,1:T(4,128)}, u32[]{:S(2)}) copy-start(f32[4096,4]{0,1:T(4,128)} %param.26) | copy-start | bytes 196612
  17.4 4.0 %copy-start.3 = (f32[1024,6,4]{0,2,1:T(4,128)S(1)}, f32[1024,6,4]{0,2,1:T(4,128)}, u32[]{:S(2)}) copy-start(f32[1024,6,4]{0,2,1:T(4,128)} %param.28) | copy-start | bytes 294916
  17.4 4.0 %copy-start.6 = (bf16[256,78]{0,1:T(8,128)(2,1)S(1)}, bf16[256,78]{0,1:T(8,128)(2,1)}, u32[]{:S(2)}) copy-start(bf16[256,78]{0,1:T(8,128)(2,1)} %param.40) | copy-start | bytes 119812
  22.2 5.4 %copy-start.1 = (bf16[4096,78]{1,0:T(8,128)(2,1)S(1)}, bf16[4096,78]{1,0:T(8,128)(2,1)}, u32[]{:S(2)}) copy-start(bf16[4096,78]{1,0:T(8,128)(2,1)} %get-tuple-element.28) | copy-start | bytes 1916932
  277.6 2.9 %copy-start.2 = (f32[4096,78]{1,0:T(8,128)S(1)}, f32[4096,78]{1,0:T(8,128)}, u32[]{:S(2)}) copy-start(f32[4096,78]{1,0:T(8,128)} %get-tuple-element.9) | copy-start | bytes 3833860

commit v4 on v3

--- a/solution.py
+++ b/solution.py
@@ -21,6 +21,10 @@
     return jnp.dot(a, b, preferred_element_type=F32)
 
 
+def dot_t(a, b):
+    return lax.dot_general(a, b, (((1,), (1,)), ((), ())), preferred_element_type=F32)
+
+
 def silu_of_half(half):
     return (half * jnp.tanh(half) + half).astype(BF16)
 
@@ -57,17 +61,23 @@
         for j in range(8):
             for i in range(8):
                 perm[r * 64 + j * 8 + i, (i * 8 + j) * 4 + r] = 1.0
-    return np.stack([perm, perm.T])
+    swap = np.zeros((256, 256), np.float32)
+    for g in range(4):
+        for j in range(8):
+            for i in range(8):
+                swap[g * 64 + j * 8 + i, g * 64 + i * 8 + j] = 1.0
+    return np.stack([perm, perm.T, swap])
 
 
 def solution(mesh):
     group = mesh.shape["gp"]
 
-    def kernel(f0, xc_hbm, ef_hbm, mf, stats, perms, wg, wemb, wembo, wei_hbm, weo_hbm, wni_hbm, wno_hbm, wgs, woh, wof,
+    def kernel(xp_hbm, xc_hbm, force_t, static_t, g2m_t, m2g_t, mesh_t, edge_t, stats, perms, w_grid, w_mesh, w_eemb, wembo, wei_hbm, weo_hbm, wni_hbm, wno_hbm, wgs, woh, wof,
                out0, out1,
                wei, weo, wni, wno, xst, xs, fm, g2m, m2g, glat, gcur, mlat, efl, ebase, elat, hsend, hin, hcur, hd,
                proj, recv, halo_s, halo_r, stage, wsh,
-               wsem, xsem, osem, ef_s, ef_r, en_s, en_r, de_s, de_r, ha_s, ha_r):
+               wg, wemb, wg32, wemb32, w32, mis, msc, esc, gsnd, msnd, ghalo, mhalo, eft,
+               wsem, xsem, sh_s, sh_r, osem, ef_s, ef_r, en_s, en_r, de_s, de_r, ha_s, ha_r):
         me = lax.axis_index("gp")
         left = lax.rem(me + group - 1, group)
         right = lax.rem(me + 1, group)
@@ -80,11 +90,64 @@
 
         weight_copies = [pltpu.make_async_copy(src, dst, wsem.at[i]) for i, (src, dst) in enumerate(
             [(wei_hbm, wei), (weo_hbm, weo), (wni_hbm, wni), (wno_hbm, wno)])]
-        x_copy = pltpu.make_async_copy(xc_hbm, xst.at[0], xsem)
-        x_copy.start()
+        x_copies = [pltpu.make_async_copy(src, xst.at[i], xsem.at[i]) for i, src in enumerate((xc_hbm, xp_hbm))]
+        for copy in x_copies:
+            copy.start()
         for copy in weight_copies:
             copy.start()
+        grid_dev = xst.shape[2]
+        variables = xst.shape[1]
+        half_grid = grid_dev // 2
+        half_mesh = mesh_t.shape[1] // 2
+        gsnd[0:g2m_t.shape[0], :] = g2m_t[:, 0:half_grid]
+        msnd[0:mesh_t.shape[0], :] = mesh_t[:, 0:half_mesh]
+        shift_copies = [pltpu.make_async_remote_copy(
+            src_ref=src, dst_ref=dst, send_sem=sh_s.at[i], recv_sem=sh_r.at[i], device_id={"gp": left}, device_id_type=MESH_ID)
+            for i, (src, dst) in enumerate(((gsnd, ghalo), (msnd, mhalo)))]
+
+        mis[...] = jnp.zeros(mis.shape, F32)
+        msc[...] = jnp.zeros(msc.shape, F32)
+        esc[...] = jnp.zeros(esc.shape, F32)
+        force = force_t.shape[0]
+        for f in range(force):
+            mis[8 * f:8 * f + 2, :] = force_t[f]
+        mis[24:24 + static_t.shape[0], :] = static_t[...]
+        mis[32:32 + m2g_t.shape[0], :] = m2g_t[...]
+        mis[40:40 + g2m_t.shape[0], 0:half_grid] = g2m_t[:, half_grid:]
+        msc[0:mesh_t.shape[0], 0:half_mesh] = mesh_t[:, half_mesh:]
+        for k in range(6):
+            esc[8 * k:8 * k + edge_t.shape[1], :] = edge_t[k]
+
+        w32[0:w_grid.shape[0], :] = w_grid[...].astype(F32) * 0.5
+        wg32[...] = jnp.zeros(wg32.shape, F32)
+        wemb32[...] = jnp.zeros(wemb32.shape, F32)
+        for s in range(2):
+            wg32[s, 0:variables, :] = w32[0:variables, :]
+            wg32[s, 128:128 + variables, :] = w32[variables:2 * variables, :]
+            for f in range(force):
+                wg32[s, 256 + 8 * f + s:257 + 8 * f + s, :] = w32[2 * variables + f:2 * variables + f + 1, :]
+            for f in range(static_t.shape[0]):
+                at = 2 * variables + force + f
+                wg32[s, 280 + f:281 + f, :] = w32[at:at + 1, :]
+            wg[s] = wg32[s].astype(BF16)
+        places = [(40, w_eemb[0]), (32, w_eemb[1]), (0, w_mesh[...])] + [(8 * k, w_eemb[2]) for k in range(6)]
+        for i, (at, rows) in enumerate(places):
+            wemb32[i, at:at + rows.shape[0], :] = rows.astype(F32) * 0.5
+            wemb[i] = wemb32[i].astype(BF16)
+
+        def wide(rows):
+            return jnp.concatenate([rows, jnp.zeros((128 - rows.shape[0], rows.shape[1]), F32)], axis=0).astype(BF16)
+
+        for q in range(4):
+            feats = dot_t(perms[2], wide(esc[:, q * 256:q * 256 + 256])).astype(BF16)
+            for g in range(4):
+                chunk = 4 * q + g
+                eft[chunk // group, chunk % group] = feats[g * 64:g * 64 + 64]
+        for slot in range(3):
+            xs[slot] = jnp.zeros(xs.shape[1:], BF16)
         pl.semaphore_wait(barrier, group - 1)
+        for copy in shift_copies:
+            copy.start()
 
         def block_of(device, half):
             return lax.rem(2 * device + half, blocks)
@@ -92,25 +155,31 @@
         def ef_copy(hop, half):
             dest = lax.rem(me + hop, group)
             return pltpu.make_async_remote_copy(
-                src_ref=ef_hbm.at[half, dest], dst_ref=efl.at[2 * me + half], send_sem=ef_s.at[dest, half],
+                src_ref=eft.at[half, dest], dst_ref=efl.at[2 * me + half], send_sem=ef_s.at[dest, half],
                 recv_sem=ef_r.at[me, half], device_id={"gp": dest}, device_id_type=MESH_ID)
 
         def ef_keep(half):
-            return pltpu.make_async_copy(ef_hbm.at[half, me], efl.at[2 * me + half], ef_r.at[me, half])
+            return pltpu.make_async_copy(eft.at[half, me], efl.at[2 * me + half], ef_r.at[me, half])
 
         for half in range(2):
             for hop in range(1, group):
                 ef_copy(hop, half).start()
             ef_keep(half).start()
 
+        for copy in x_copies:
+            copy.wait()
+        mean = stats[:, 0:1]
+        std = stats[:, 1:2]
+
         def embed_task(rows):
-            feats = dot(perms[0], f0[rows, :])
-            yield
-            feats = feats.astype(BF16)
-            xs[0, rows, :] = feats[:, 0:128]
-            xs[1, rows, :] = feats[:, 128:256]
-            misc = feats[:, 256:384]
+            misc = dot_t(perms[0], wide(mis[:, rows]))
+            prev = dot_t(perms[0], ((xst[1, :, rows] - mean) / std).astype(BF16))
+            cur = dot_t(perms[0], ((xst[0, :, rows] - mean) / std).astype(BF16))
+            yield
+            misc = misc.astype(BF16)
             fm[rows, :] = misc
+            xs[0, rows, 0:variables] = prev.astype(BF16)
+            xs[1, rows, 0:variables] = cur.astype(BF16)
             first = dot(misc, wemb[0])
             second = dot(misc, wemb[1])
             yield
@@ -124,7 +193,14 @@
             together(embed_task(pl.ds(pl.multiple_of((it * 4 + sub) * 256, 256), 256)) for sub in range(4))
             return carry
 
-        lax.fori_loop(0, 4, embed_rows, 0)
+        lax.fori_loop(0, 2, embed_rows, 0)
+        for copy in shift_copies:
+            copy.wait_recv()
+        mis[40:40 + g2m_t.shape[0], half_grid:] = ghalo[0:g2m_t.shape[0], :]
+        msc[0:mesh_t.shape[0], half_mesh:] = mhalo[0:mesh_t.shape[0], :]
+        lax.fori_loop(2, 4, embed_rows, 0)
+        for copy in shift_copies:
+            copy.wait_send()
 
         def plain_task(get, put, w_first, w_second):
             y = dot(get(), w_first)
@@ -136,10 +212,10 @@
         def mesh_task(rows):
             def put(y):
                 mlat[rows, :] = y.astype(BF16)
-            return plain_task(lambda: mf[rows, :], put, wemb[2], wembo[1])
-
-        together(mesh_task(pl.ds(sub * 256, 256)) for sub in range(4))
-        xs[2] = jnp.zeros(xs.shape[1:], BF16)
+            feats = dot_t(perms[2], wide(msc[:, rows])).astype(BF16)
+            return plain_task(lambda: feats, put, wemb[2], wembo[1])
+
+        together(mesh_task(slice(sub * 256, sub * 256 + 256)) for sub in range(4))
         for copy in weight_copies:
             copy.wait()
 
@@ -176,7 +252,7 @@
 
         def ef_arrival(source, half):
             return pltpu.make_async_remote_copy(
-                src_ref=ef_hbm.at[half, me], dst_ref=efl.at[2 * source + half], send_sem=ef_s.at[me, half],
+                src_ref=eft.at[half, me], dst_ref=efl.at[2 * source + half], send_sem=ef_s.at[me, half],
                 recv_sem=ef_r.at[source, half], device_id={"gp": left}, device_id_type=MESH_ID)
 
         def halo_copies(slot):
@@ -379,10 +455,6 @@
 
             lax.fori_loop(0, 4, self_update, 0)
 
-            @pl.when(step == 0)
-            def _():
-                x_copy.wait()
-
             def decode(it, carry):
                 last = layers - 1
                 for q in range(PER - 1):
@@ -399,7 +471,7 @@
                     source = lax.rem(me + PER * it + 1 + q, group)
                     for half in range(2):
                         rows = pl.ds(pl.multiple_of((half * group + source) * 256, 256), 256)
-                        work.append((rows, hd[half, source], m2g[rows, :], gcur[rows, :], xst[step, rows, :]))
+                        work.append((rows, hd[half, source], m2g[rows, :], gcur[rows, :], xst[step, :, rows]))
                 def decode_task(rows, node, old, grid, state):
                     pre = dot(old, wei[last, 0:256, :]) + dot(grid, wei[last, 512:768, :])
                     term = dot(node, wei[last, 256:512, :])
@@ -417,13 +489,13 @@
                     yield
                     hidden = dot(perms[1], silu_of_half(pre))
                     yield
-                    p = dot(hidden.astype(BF16), wof[...])
-                    yield
-                    new = state + stats[3:4, :] * p + stats[2:3, :]
-                    scaled = dot(perms[0], ((new - stats[0:1, :]) / stats[1:2, :]).astype(BF16))
-                    yield
-                    xst[step + 1, rows, :] = new
-                    xs[2, rows, 0:new.shape[1]] = scaled.astype(BF16)
+                    p = dot_t(wof[...], hidden.astype(BF16))
+                    yield
+                    new = state + stats[:, 3:4] * p + stats[:, 2:3]
+                    scaled = dot_t(perms[0], ((new - mean) / std).astype(BF16))
+                    yield
+                    xst[step + 1, :, rows] = new
+                    xs[2, rows, 0:variables] = scaled.astype(BF16)
 
                 staggered((decode_task(*args) for args in work), 2 * PER)
                 return carry
@@ -444,65 +516,26 @@
         pltpu.make_async_copy(xst.at[1], out0, osem.at[0]).wait()
         final.wait()
 
-    def shift_pairs(hop_count):
-        return [(source, (source + hop_count) % group) for source in range(group)]
-
     def local_run(x_prev, x_cur, forcing, grid_static, g2m_feat, m2g_feat, mesh_feat, mesh_edge_feat, norm_stats, w_grid_in, w_mesh_in, w_eemb_in, w_embed_out, w_edge_in, w_edge_out, w_node_in, w_node_out, w_grid_self, w_out_hidden, w_out_final):
         grid_dev, variables = x_prev.shape
         mesh_dev = mesh_feat.shape[0]
         latent = w_embed_out.shape[-1]
         blocks = 2 * group
-        half_grid = grid_dev // 2
-        half_mesh = mesh_dev // 2
-
-        def shifted(values, half):
-            head = lax.ppermute(values[:half], "gp", shift_pairs(-1))
-            return jnp.concatenate([values[half:], head], axis=0)
-
-        def in_order(values):
-            lanes = values.shape[-1]
-            values = values.reshape(2, group, 8, 8, lanes).transpose(0, 1, 3, 2, 4)
-            return values.reshape(2, group, 64, lanes)
-
-        def lane_pad(values, width):
-            return jnp.pad(values, [(0, 0)] * (values.ndim - 1) + [(0, width - values.shape[-1])])
-
-        g2m_here = shifted(g2m_feat, half_grid)
-        mesh_here = shifted(mesh_feat, half_mesh)
-        misc = jnp.concatenate([forcing[:, 0, :], forcing[:, 1, :], grid_static, g2m_here, m2g_feat], axis=1)
-        force = forcing.shape[-1]
-        static = grid_static.shape[-1]
-        edge_lanes = g2m_feat.shape[-1]
-        scale = lambda x: (x - norm_stats[0]) / norm_stats[1]
-        feats = jnp.concatenate([lane_pad(scale(x_prev), 128), lane_pad(scale(x_cur), 128), lane_pad(misc, 128)], axis=1).astype(BF16)
-        mesh_rows = lane_pad(in_order(mesh_here).astype(BF16), 128).reshape(mesh_dev, 128)
-        edge_rows = lane_pad(in_order(mesh_edge_feat.reshape(mesh_dev, -1)).astype(BF16), 128)
-
-        def placed(rows, start, height):
-            return jnp.pad(rows, ((start, height - start - rows.shape[0]), (0, 0)))
-
-        w_force = w_grid_in[2 * variables:2 * variables + force]
-        w_static = w_grid_in[2 * variables + force:]
-        w_state = placed(w_grid_in[:variables], 0, 384) + placed(w_grid_in[variables:2 * variables], 128, 384) + placed(w_static, 256 + 2 * force, 384)
-        w_grid = 0.5 * jnp.stack([w_state + placed(w_force, 256 + force * s, 384) for s in range(2)])
-        at_g2m = 2 * force + static
-        w_embed = 0.5 * jnp.stack([placed(w_eemb_in[0], at_g2m, 128), placed(w_eemb_in[1], at_g2m + edge_lanes, 128), placed(w_mesh_in, 0, 128)]
-                            + [placed(w_eemb_in[2], edge_lanes * k, 128) for k in range(6)])
         perms = jnp.asarray(row_permutation(), BF16)
 
         vmem = pl.BlockSpec(memory_space=pltpu.VMEM)
         anywhere = pl.BlockSpec(memory_space=pl.ANY)
-        state = jax.ShapeDtypeStruct((grid_dev, variables), F32)
+        state = jax.ShapeDtypeStruct((variables, grid_dev), F32)
         dma = pltpu.SemaphoreType.DMA
-        return pl.pallas_call(
+        first, second = pl.pallas_call(
             kernel,
             out_shape=(state, state),
-            in_specs=[vmem, anywhere, anywhere] + [vmem] * 6 + [anywhere] * 4 + [vmem] * 3,
+            in_specs=[anywhere, anywhere] + [vmem] * 12 + [anywhere] * 4 + [vmem] * 3,
             out_specs=(anywhere, anywhere),
             scratch_shapes=[
                 pltpu.VMEM(w_edge_in.shape, BF16), pltpu.VMEM(w_edge_out.shape, BF16),
                 pltpu.VMEM(w_node_in.shape, BF16), pltpu.VMEM(w_node_out.shape, BF16),
-                pltpu.VMEM((3, grid_dev, variables), F32), pltpu.VMEM((3, grid_dev, 128), BF16), pltpu.VMEM((grid_dev, 128), BF16),
+                pltpu.VMEM((3, variables, grid_dev), F32), pltpu.VMEM((3, grid_dev, 128), BF16), pltpu.VMEM((grid_dev, 128), BF16),
                 pltpu.VMEM((grid_dev, latent), BF16), pltpu.VMEM((grid_dev, latent), BF16), pltpu.VMEM((grid_dev, latent), BF16),
                 pltpu.VMEM((grid_dev, latent), BF16),
                 pltpu.VMEM((mesh_dev, latent), BF16), pltpu.VMEM((blocks, 64, 128), BF16),
@@ -511,12 +544,19 @@
                 pltpu.VMEM((blocks, 64, latent), BF16), pltpu.VMEM((2, group, 64, latent), BF16),
                 pltpu.VMEM((blocks, 80, latent), F32), pltpu.VMEM((mesh_dev, latent), F32),
                 pltpu.VMEM((2, 2, blocks, latent), BF16), pltpu.VMEM((2, 2, blocks, latent), BF16), pltpu.VMEM((2, blocks, latent), F32), pltpu.VMEM((2, latent, latent), BF16),
-                dma((4,)), dma, dma((2,)), dma((group, 2)), dma((group, 2)), dma((group, 2)), dma((group, 2)),
+                pltpu.VMEM((2, 384, latent), BF16), pltpu.VMEM((9, 128, latent), BF16), pltpu.VMEM((2, 384, latent), F32),
+                pltpu.VMEM((9, 128, latent), F32), pltpu.VMEM((-(-w_grid_in.shape[0] // 8) * 8, latent), F32),
+                pltpu.VMEM((64, grid_dev), F32), pltpu.VMEM((8, mesh_dev), F32), pltpu.VMEM((48, mesh_dev), F32),
+                pltpu.VMEM((8, grid_dev // 2), F32), pltpu.VMEM((8, mesh_dev // 2), F32), pltpu.VMEM((8, grid_dev // 2), F32),
+                pltpu.VMEM((8, mesh_dev // 2), F32), pltpu.VMEM((2, group, 64, 128), BF16),
+                dma((4,)), dma((2,)), dma((2,)), dma((2,)), dma((2,)), dma((group, 2)), dma((group, 2)), dma((group, 2)), dma((group, 2)),
                 dma((group, 2)), dma((group, 2)), dma((2, 2)), dma((2, 2)),
             ],
             compiler_params=pltpu.CompilerParams(collective_id=0, has_side_effects=True, flags=FLAGS, vmem_limit_bytes=67043328),
-        )(feats, x_cur, edge_rows, mesh_rows, norm_stats, perms, w_grid, w_embed, w_embed_out, w_edge_in, w_edge_out, w_node_in, w_node_out,
-          w_grid_self, w_out_hidden, w_out_final)
+        )(x_prev.T, x_cur.T, forcing.transpose(2, 1, 0), grid_static.T, g2m_feat.T, m2g_feat.T, mesh_feat.T, mesh_edge_feat.transpose(1, 2, 0),
+          norm_stats.T, perms, w_grid_in, w_mesh_in, w_eemb_in, w_embed_out, w_edge_in, w_edge_out, w_node_in, w_node_out, w_grid_self,
+          w_out_hidden, w_out_final.T)
+        return first.T, second.T
 
     row_spec = P(("dp", "gp"))
     edge_spec = P(("dp", "gp"), None, None)

time: 283 us -> 259 us (0.915)
  local copies, waits for them, and re-layouts: 22.3 us -> 5.03 us
  other arithmetic: 6.88 us -> 0 us
  Pallas kernels: 248 us -> 254 us
  starting transfers between devices: 4.15 us -> 0 us
    pallas_call x1, Pallas kernels: 248 us -> 254 us  [local_run(): pl.pallas_call(kernel, out_shape=(state, state), in_specs=[anywhere, anyw...]
    pallas_call x2 -> x0, local copies, waits for them, and re-layouts: 4.62 us -> none  [local_run(): pl.pallas_call(kernel, out_shape=(state, state), in_specs=[vmem, anywhere...]
    ppermute x2 -> x0, starting transfers between devices: 4.15 us -> none  [shifted(): head = lax.ppermute(values[:half], 'gp', shift_pairs(-1))]
    another operation x4 -> x0, other arithmetic: 3.16 us -> none
    slice x4 -> x0, local copies, waits for them, and re-layouts: 3.15 us -> none  [the longest x2 1.51 us: shifted(): return jnp.concatenate([values[half:], head], axis=0)]
    unnamed x26 -> x5, local copies, waits for them, and re-layouts: 7.69 us -> 5.03 us
  transfers between devices with their start and end apart: 2 -> 0, of which waited for: 0 -> 0; matrix products, arithmetic and copies ran while one was open for 7% -> 0% of each run, Pallas kernels for 0% -> 0%
where the time goes in v4:
time: 259 us
  Pallas kernels  254 us (98%)
  local copies, waits for them, and re-layouts  5.03 us (2%)
    pallas_call x1, Pallas kernels, local_run(): pl.pallas_call(kernel, out_shape=(state, state), in_specs=[anywhere, anyw...  254 us

profile of v4, /device:TPU:113, one launch (start us, length us, event | category | flops | bytes accessed | tf_op | source)
XLA Modules:
  0.0 259.2 jit_solution(9135730173749951951)
XLA Ops:
  0.6 1.4 copy.23
  2.0 253.5 %shard_map.212 = (f32[78,4096]{1,0:T(8,128)}, f32[78,4096]{1,0:T(8,128)}) custom-call(f32[78,4096]{1,0:T(8,128)} %bitcast.12, f32[78,4096]{1,0:T(8,128)} %bitcast.13, f32[3,2,4096]{2,1,0:T(2,128)} %bitcast.17, f32[3,4096]{1,0:T(4,128)} %bitcast.19, f32[4,4096]{1,0:T(4,128)} %bitcast.20, f32[4,4096]{1,0:T(4,128)} %bitcast.21, f32[3,1024]{1,0:T(4,128)} %bitcast.23, ...), custom_call_target="tpu_custom_call" | custom-call | tf_op jit(solution)/shard_map/pallas_call | solution.py:530
  255.6 0.0 copy-start
  255.6 2.6 copy.26
  258.2 0.0 copy-done
  258.2 1.1 copy.27
Async XLA Ops:
  255.6 2.6 copy-start

commit v5 on v4

--- a/solution.py
+++ b/solution.py
@@ -10,10 +10,9 @@
 F32 = jnp.float32
 BF16 = jnp.bfloat16
 SUB = 256
-TAIL = 256
 PER = 4
 WIDTH = 3
-TAIL_WIDTH = 4
+TAIL_WIDTH = 6
 FLAGS = {}
 
 
@@ -75,7 +74,7 @@
     def kernel(xp_hbm, xc_hbm, force_t, static_t, g2m_t, m2g_t, mesh_t, edge_t, stats, perms, w_grid, w_mesh, w_eemb, wembo, wei_hbm, weo_hbm, wni_hbm, wno_hbm, wgs, woh, wof,
                out0, out1,
                wei, weo, wni, wno, xst, xs, fm, g2m, m2g, glat, gcur, mlat, efl, ebase, elat, hsend, hin, hcur, hd,
-               proj, recv, halo_s, halo_r, stage, wsh,
+               proj, recv, halo_s, halo_r, stage, wsh, hb, efj,
                wg, wemb, wg32, wemb32, w32, mis, msc, esc, gsnd, msnd, ghalo, mhalo, eft,
                wsem, xsem, sh_s, sh_r, osem, ef_s, ef_r, en_s, en_r, de_s, de_r, ha_s, ha_r):
         me = lax.axis_index("gp")
@@ -237,7 +236,7 @@
         def de_copy(hop, half):
             dest = lax.rem(me + hop, group)
             return pltpu.make_async_remote_copy(
-                src_ref=hcur.at[block_of(dest, 1 + half)], dst_ref=hd.at[half, me], send_sem=de_s.at[dest, half],
+                src_ref=hb.at[block_of(dest, 1 + half)], dst_ref=hd.at[half, me], send_sem=de_s.at[dest, half],
                 recv_sem=de_r.at[me, half], device_id={"gp": dest}, device_id_type=MESH_ID)
 
         def en_arrival(source, half):
@@ -247,7 +246,7 @@
 
         def de_arrival(source, half):
             return pltpu.make_async_remote_copy(
-                src_ref=hcur.at[0], dst_ref=hd.at[half, source], send_sem=de_s.at[me, half],
+                src_ref=hb.at[0], dst_ref=hd.at[half, source], send_sem=de_s.at[me, half],
                 recv_sem=de_r.at[source, half], device_id={"gp": left}, device_id_type=MESH_ID)
 
         def ef_arrival(source, half):
@@ -255,93 +254,104 @@
                 src_ref=eft.at[half, me], dst_ref=efl.at[2 * source + half], send_sem=ef_s.at[me, half],
                 recv_sem=ef_r.at[source, half], device_id={"gp": left}, device_id_type=MESH_ID)
 
-        def halo_copies(slot):
-            return [pltpu.make_async_remote_copy(
+        def halo_copy(slot, side):
+            return pltpu.make_async_remote_copy(
                 src_ref=halo_s.at[slot, side], dst_ref=halo_r.at[slot, 1 - side], send_sem=ha_s.at[slot, side],
                 recv_sem=ha_r.at[slot, 1 - side], device_id={"gp": (left, right)[side]}, device_id_type=MESH_ID)
-                for side in range(2)]
-
-        def send_halo(slot):
+
+        def wait_halo(slot):
+            for side in range(2):
+                halo_copy(slot, 1 - side).wait_recv()
+            for side in range(2):
+                halo_copy(slot, side).wait_send()
+
+        def send_halo(slot, side, rows):
             for b in range(blocks):
-                stage[0, b:b + 1, :] = hcur[b, 0:16, :].astype(F32)[0:1]
-                stage[1, b:b + 1, :] = hcur[b, 48:64, :].astype(F32)[15:16]
-            halo_s[slot, 0] = stage[0].astype(BF16)
-            halo_s[slot, 1] = stage[1].astype(BF16)
-            for copy in halo_copies(slot):
-                copy.start()
-
-        def edge_task(layer, k, sub, size, send):
+                at = 8 * b + 7 * side
+                stage[2 + side, b:b + 1, :] = rows[at:at + 1]
+            halo_s[slot, side] = stage[2 + side].astype(BF16)
+            halo_copy(slot, side).start()
+
+        def by_j(values):
+            return jnp.concatenate([values[:, 8 * j:8 * j + 8, :].reshape(blocks * 8, values.shape[-1]) for j in range(8)], axis=0)
+
+        def by_block(values):
+            values = values.reshape(8, blocks, 8, values.shape[-1])
+            return jnp.stack([values[:, b].reshape(64, values.shape[-1]) for b in range(blocks)], axis=0)
+
+        span = blocks * 8
+
+        def rolled(shift, sub, size):
+            cut = shift % blocks * 8
+            pieces = []
+            for base in range(sub + span, sub + size + span, span):
+                pieces += [proj[base + cut:base + span, :], proj[base:base + cut, :]]
+            return jnp.concatenate(pieces, axis=0)
+
+        def edge_send(k, sub, size):
+            if k == 0:
+                return proj[sub + 2 * span:sub + 2 * span + size, :]
+            if k == 1:
+                return proj[sub:sub + size, :]
+            return rolled((1, -1, 4, -4)[k - 2], sub, size)
+
+        def edge_task(layer, k, sub, size):
             rows = slice(sub, sub + size)
             old = elat[k, rows, :]
-            pre = dot(old, wei[layer, 0:256, :]) + (send + recv[rows, :])
+            pre = dot(old, wei[layer, 0:256, :]) + (edge_send(k, sub, size) + recv[rows, :])
             yield
             y = dot(silu_of_half(pre), weo[layer])
             yield
             elat[k, rows, :] = residual(old, norm(y))
 
-        def project(layer, lo, hi):
-            h = hcur[lo:hi].reshape((hi - lo) * 64, 256)
-            return dot(h, wei[layer, 256:512, :]), dot(h, wei[layer, 512:768, :])
-
-        def put_projections(lo, hi, send, receive):
-            proj[lo:hi, 8:72, :] = send.reshape(hi - lo, 64, 256)
-            recv[lo * 64:hi * 64, :] = receive
-
-        def tail_task(layer, lo, hi):
-            size = (hi - lo) * 64
-            rows = slice(lo * 64, hi * 64)
-            olds = [elat[k, rows, :] for k in range(2)]
-            sends = [proj[lo:hi, 16:80, :].reshape(size, 256), proj[lo:hi, 0:64, :].reshape(size, 256)]
-            pres = [dot(old, wei[layer, 0:256, :]) + (send + recv[rows, :]) for old, send in zip(olds, sends)]
-            total = elat[2, rows, :].astype(F32)
-            for k in range(3, 6):
+        def put_projections(rows, send, receive):
+            proj[rows.start + span:rows.stop + span, :] = send
+            recv[rows, :] = receive
+
+        def node_task(layer, sub, size):
+            rows = slice(sub, sub + size)
+            total = elat[0, rows, :].astype(F32)
+            for k in range(1, 6):
                 total = total + elat[k, rows, :].astype(F32)
-            yield
-            ys = [dot(silu_of_half(pre), weo[layer]) for pre in pres]
-            yield
-            for k in range(2):
-                new = residual(olds[k], norm(ys[k]))
-                elat[k, rows, :] = new
-                total = total + new.astype(F32)
-            node = hcur[lo:hi].reshape(size, 256)
+            node = hcur[rows, :]
             pre = dot(node, wni[layer, 0:256, :]) + dot(total.astype(BF16), wni[layer, 256:512, :])
             yield
             y = dot(silu_of_half(pre), wno[layer])
             yield
             new = residual(node, norm(y))
-            hcur[lo:hi] = new.reshape(hi - lo, 64, 256)
+            hcur[rows, :] = new
             send = dot(new, wei[layer + 1, 256:512, :])
             receive = dot(new, wei[layer + 1, 512:768, :])
-            yield
-            put_projections(lo, hi, send, receive)
-
-        def rolled(shift, sub, size):
-            lo, count = sub // 64, size // 64
-            picks = [(lo + q + shift) % blocks for q in range(count)]
-            return jnp.concatenate([proj[b, 8:72, :] for b in picks], axis=0)
+            next_slot = lax.rem(layer + 1, 2)
+            if sub == 0:
+                send_halo(next_slot, 0, new[0:span].astype(F32))
+            if sub + size == 8 * span:
+                send_halo(next_slot, 1, new[size - span:size].astype(F32))
+            yield
+            put_projections(rows, send, receive)
 
         def mesh_layer(layer, carry):
             slot = lax.rem(layer, 2)
-            staggered((edge_task(layer, k, sub, SUB, rolled(shift, sub, SUB))
-                       for k, shift in ((2, 1), (3, -1), (4, 4), (5, -4)) for sub in range(0, blocks * 64, SUB)), WIDTH)
-            for copy in halo_copies(slot):
-                copy.wait_recv()
-            for copy in halo_copies(slot):
-                copy.wait_send()
-            edge_proj = dot(halo_r[slot].reshape(32, 256), wei[layer, 256:512, :])
-            low = edge_proj[0:16]
-            high = edge_proj[16:32]
-            stage[0] = jnp.where(me == 0, jnp.concatenate([low[15:16], low[0:15]], axis=0), low)
-            stage[1] = jnp.where(me == group - 1, jnp.concatenate([high[1:16], high[0:1]], axis=0), high)
-            sublane = lax.broadcasted_iota(jnp.int32, (8, 256), 0)
             for b in range(blocks):
-                proj[b, 0:8, :] = jnp.where(sublane == 0, stage[0, b:b + 1, :], pltpu.roll(proj[b, 64:72, :], 1, 0))
-                proj[b, 72:80, :] = jnp.where(sublane == 7, stage[1, b:b + 1, :], pltpu.roll(proj[b, 8:16, :], 7, 0))
-            staggered((tail_task(layer, lo, lo + TAIL // 64) for lo in range(0, blocks, TAIL // 64)), TAIL_WIDTH)
-
-            @pl.when(layer < layers - 2)
-            def _():
-                send_halo(1 - slot)
+                proj[8 * b:8 * b + 8, :] = pltpu.roll(proj[8 * span + 8 * b:8 * span + 8 * b + 8, :], 1, 0)
+                proj[9 * span + 8 * b:9 * span + 8 * b + 8, :] = pltpu.roll(proj[span + 8 * b:span + 8 * b + 8, :], 7, 0)
+            size = 2 * span
+            subs = range(0, 8 * span, size)
+            early = [(k, sub) for k in (2, 3, 4, 5) for sub in subs]
+            early += [(0, sub) for sub in subs[:-1]] + [(1, sub) for sub in subs[1:]]
+            staggered((edge_task(layer, k, sub, size) for k, sub in early), WIDTH)
+            wait_halo(slot)
+            edge_proj = dot(halo_r[slot].reshape(2 * blocks, 256), wei[layer, 256:512, :])
+            low = edge_proj[0:blocks]
+            high = edge_proj[blocks:2 * blocks]
+            stage[0] = jnp.where(me == 0, jnp.concatenate([low[blocks - 1:], low[:blocks - 1]], axis=0), low)
+            stage[1] = jnp.where(me == group - 1, jnp.concatenate([high[1:], high[:1]], axis=0), high)
+            for b in range(blocks):
+                proj[8 * b:8 * b + 1, :] = stage[0, b:b + 1, :]
+                proj[9 * span + 8 * b + 7:9 * span + 8 * b + 8, :] = stage[1, b:b + 1, :]
+            tasks = [edge_task(layer, 1, 0, size), edge_task(layer, 0, subs[-1], size)]
+            tasks += [node_task(layer, sub, size) for sub in (subs[1], subs[0], subs[-1], subs[2])]
+            staggered(tasks, TAIL_WIDTH)
             return carry
 
         def forecast(step, carry):
@@ -409,11 +419,13 @@
                         ef_arrival(lax.rem(me + hop, group), half).wait_recv()
                     ef_keep(half).wait()
 
+                efj[...] = by_j(efl[...].astype(F32)).astype(BF16)
+
                 def embed_edges(k, carry):
                     def edge_embed_task(sub):
                         def put(y):
                             ebase[k, sub * 64:sub * 64 + 256, :] = y.astype(BF16)
-                        return plain_task(lambda: efl[sub:sub + 4].reshape(256, 128), put, wemb[3 + k], wembo[4])
+                        return plain_task(lambda: efj[sub * 64:sub * 64 + 256, :], put, wemb[3 + k], wembo[4])
 
                     together(edge_embed_task(sub) for sub in range(0, blocks, 4))
                     return carry
@@ -430,17 +442,21 @@
             for hop in range(1, group):
                 for half in range(2):
                     en_copy(hop, half).wait_send()
-            hcur[...] = hin[...]
             for half in range(2):
-                hcur[block_of(me, 1 + half)] = hsend[half, me]
-            send_halo(1)
-            put_projections(0, blocks, *project(1, 0, blocks))
+                hin[block_of(me, 1 + half)] = hsend[half, me]
+            start = by_j(hin[...].astype(F32))
+            send_halo(1, 0, start[0:span])
+            send_halo(1, 1, start[7 * span:])
+            start = start.astype(BF16)
+            hcur[...] = start
+            put_projections(slice(0, 8 * span), dot(start, wei[1, 256:512, :]), dot(start, wei[1, 512:768, :]))
             lax.fori_loop(1, layers - 1, mesh_layer, 0)
+            hb[...] = by_block(hcur[...].astype(F32)).astype(BF16)
             for hop in range(1, group):
                 for half in range(2):
                     de_copy(hop, half).start()
             for half in range(2):
-                hd[half, me] = hcur[block_of(me, 1 + half)]
+                hd[half, me] = hb[block_of(me, 1 + half)]
 
             def self_task(rows):
                 old = glat[rows, :]
@@ -501,6 +517,7 @@
                 return carry
 
             lax.fori_loop(0, group // PER, decode, 0)
+            wait_halo(1)
             for hop in range(1, group):
                 for half in range(2):
                     de_copy(hop, half).wait_send()
@@ -541,9 +558,10 @@
                 pltpu.VMEM((mesh_dev, latent), BF16), pltpu.VMEM((blocks, 64, 128), BF16),
                 pltpu.VMEM((6, mesh_dev, latent), BF16), pltpu.VMEM((6, mesh_dev, latent), BF16),
                 pltpu.VMEM((2, group, 64, latent), BF16), pltpu.VMEM((blocks, 64, latent), BF16),
-                pltpu.VMEM((blocks, 64, latent), BF16), pltpu.VMEM((2, group, 64, latent), BF16),
-                pltpu.VMEM((blocks, 80, latent), F32), pltpu.VMEM((mesh_dev, latent), F32),
-                pltpu.VMEM((2, 2, blocks, latent), BF16), pltpu.VMEM((2, 2, blocks, latent), BF16), pltpu.VMEM((2, blocks, latent), F32), pltpu.VMEM((2, latent, latent), BF16),
+                pltpu.VMEM((mesh_dev, latent), BF16), pltpu.VMEM((2, group, 64, latent), BF16),
+                pltpu.VMEM((10 * blocks * 8, latent), F32), pltpu.VMEM((mesh_dev, latent), F32),
+                pltpu.VMEM((2, 2, blocks, latent), BF16), pltpu.VMEM((2, 2, blocks, latent), BF16), pltpu.VMEM((4, blocks, latent), F32), pltpu.VMEM((2, latent, latent), BF16),
+                pltpu.VMEM((blocks, 64, latent), BF16), pltpu.VMEM((mesh_dev, 128), BF16),
                 pltpu.VMEM((2, 384, latent), BF16), pltpu.VMEM((9, 128, latent), BF16), pltpu.VMEM((2, 384, latent), F32),
                 pltpu.VMEM((9, 128, latent), F32), pltpu.VMEM((-(-w_grid_in.shape[0] // 8) * 8, latent), F32),
                 pltpu.VMEM((64, grid_dev), F32), pltpu.VMEM((8, mesh_dev), F32), pltpu.VMEM((48, mesh_dev), F32),

time: 259 us -> 267 us (1.031)
  Pallas kernels: 254 us -> 261 us
    pallas_call x1, Pallas kernels: 254 us -> 261 us  [local_run(): pl.pallas_call(kernel, out_shape=(state, state), in_specs=[anywhere, anyw...]
where the time goes in v5:
time: 267 us
  Pallas kernels  261 us (98%)
  local copies, waits for them, and re-layouts  5.03 us (2%)
    pallas_call x1, Pallas kernels, local_run(): pl.pallas_call(kernel, out_shape=(state, state), in_specs=[anywhere, anyw...  261 us

profile of v5, /device:TPU:113, one launch (start us, length us, event | category | flops | bytes accessed | tf_op | source)
XLA Modules:
  0.0 267.1 jit_solution(417173889159642034)
XLA Ops:
  0.6 1.4 copy.23
  2.0 261.4 %shard_map.212 = (f32[78,4096]{1,0:T(8,128)}, f32[78,4096]{1,0:T(8,128)}) custom-call(f32[78,4096]{1,0:T(8,128)} %bitcast.12, f32[78,4096]{1,0:T(8,128)} %bitcast.13, f32[3,2,4096]{2,1,0:T(2,128)} %bitcast.17, f32[3,4096]{1,0:T(4,128)} %bitcast.19, f32[4,4096]{1,0:T(4,128)} %bitcast.20, f32[4,4096]{1,0:T(4,128)} %bitcast.21, f32[3,1024]{1,0:T(4,128)} %bitcast.23, ...), custom_call_target="tpu_custom_call" | custom-call | tf_op jit(solution)/shard_map/pallas_call | solution.py:547
  263.4 0.0 copy-start
  263.4 2.6 copy.26
  266.0 0.0 copy-done
  266.0 1.1 copy.27
Async XLA Ops:
  263.4 2.6 copy-start

commit v6 on v4

--- a/solution.py
+++ b/solution.py
@@ -459,16 +459,16 @@
                 last = layers - 1
                 for q in range(PER - 1):
                     for half in range(2):
-                        de_arrival(lax.rem(me + PER * it + 1 + q, group), half).wait_recv()
+                        de_arrival(lax.rem(me + 2 * group - PER * it - 1 - q, group), half).wait_recv()
 
                 @pl.when(it < group // PER - 1)
                 def _():
                     for half in range(2):
-                        de_arrival(lax.rem(me + PER * it + PER, group), half).wait_recv()
+                        de_arrival(lax.rem(me + 2 * group - PER * it - PER, group), half).wait_recv()
 
                 work = []
                 for q in range(PER):
-                    source = lax.rem(me + PER * it + 1 + q, group)
+                    source = lax.rem(me + 2 * group - PER * it - 1 - q, group)
                     for half in range(2):
                         rows = pl.ds(pl.multiple_of((half * group + source) * 256, 256), 256)
                         work.append((rows, hd[half, source], m2g[rows, :], gcur[rows, :], xst[step, :, rows]))

time: 259 us -> 262 us (1.012)
    pallas_call x1, Pallas kernels: 254 us -> 256 us  [local_run(): pl.pallas_call(kernel, out_shape=(state, state), in_specs=[anywhere, anyw...]
where the time goes in v6:
time: 262 us
  Pallas kernels  256 us (98%)
  local copies, waits for them, and re-layouts  5.03 us (2%)
    pallas_call x1, Pallas kernels, local_run(): pl.pallas_call(kernel, out_shape=(state, state), in_specs=[anywhere, anyw...  256 us

profile of v6, /device:TPU:113, one launch (start us, length us, event | category | flops | bytes accessed | tf_op | source)
XLA Modules:
  0.0 261.9 jit_solution(14517737461774973694)
XLA Ops:
  0.6 1.4 copy.23
  2.0 256.2 %shard_map.212 = (f32[78,4096]{1,0:T(8,128)}, f32[78,4096]{1,0:T(8,128)}) custom-call(f32[78,4096]{1,0:T(8,128)} %bitcast.12, f32[78,4096]{1,0:T(8,128)} %bitcast.13, f32[3,2,4096]{2,1,0:T(2,128)} %bitcast.17, f32[3,4096]{1,0:T(4,128)} %bitcast.19, f32[4,4096]{1,0:T(4,128)} %bitcast.20, f32[4,4096]{1,0:T(4,128)} %bitcast.21, f32[3,1024]{1,0:T(4,128)} %bitcast.23, ...), custom_call_target="tpu_custom_call" | custom-call | tf_op jit(solution)/shard_map/pallas_call | solution.py:530
  258.3 0.0 copy-start
  258.3 2.6 copy.26
  260.9 0.0 copy-done
  260.9 1.1 copy.27
Async XLA Ops:
  258.3 2.6 copy-start

commit v7 on v4

--- a/solution.py
+++ b/solution.py
@@ -10,7 +10,7 @@
 F32 = jnp.float32
 BF16 = jnp.bfloat16
 SUB = 256
-TAIL = 256
+TAIL = 512
 PER = 4
 WIDTH = 3
 TAIL_WIDTH = 4

time: 259 us -> 254 us (0.981)
  Pallas kernels: 254 us -> 248 us
    pallas_call x1, Pallas kernels: 254 us -> 248 us  [local_run(): pl.pallas_call(kernel, out_shape=(state, state), in_specs=[anywhere, anyw...]
where the time goes in v7:
time: 254 us
  Pallas kernels  248 us (98%)
  local copies, waits for them, and re-layouts  5.03 us (2%)
    pallas_call x1, Pallas kernels, local_run(): pl.pallas_call(kernel, out_shape=(state, state), in_specs=[anywhere, anyw...  248 us

profile of v7, /device:TPU:113, one launch (start us, length us, event | category | flops | bytes accessed | tf_op | source)
XLA Modules:
  0.0 253.7 jit_solution(3556916942627006567)
XLA Ops:
  0.6 1.4 copy.23
  2.0 248.0 %shard_map.212 = (f32[78,4096]{1,0:T(8,128)}, f32[78,4096]{1,0:T(8,128)}) custom-call(f32[78,4096]{1,0:T(8,128)} %bitcast.12, f32[78,4096]{1,0:T(8,128)} %bitcast.13, f32[3,2,4096]{2,1,0:T(2,128)} %bitcast.17, f32[3,4096]{1,0:T(4,128)} %bitcast.19, f32[4,4096]{1,0:T(4,128)} %bitcast.20, f32[4,4096]{1,0:T(4,128)} %bitcast.21, f32[3,1024]{1,0:T(4,128)} %bitcast.23, ...), custom_call_target="tpu_custom_call" | custom-call | tf_op jit(solution)/shard_map/pallas_call | solution.py:530
  250.0 0.0 copy-start
  250.0 2.6 %copy.26 = f32[4096,78]{0,1:T(8,128)} copy(f32[4096,78]{0,1:T(8,128)} %bitcast.15) | data formatting | bytes 2555904
  252.6 0.0 copy-done
  252.6 1.1 copy.27
Async XLA Ops:
  250.0 2.6 %copy-start = (f32[78,4096]{1,0:T(8,128)S(1)}, f32[78,4096]{1,0:T(8,128)}, u32[]{:S(2)}) copy-start(f32[78,4096]{1,0:T(8,128)} %get-tuple-element.5) | copy-start | bytes 3833860
